TPU v7x, 32 devices: a whole 2x2x4 slice. The times are simulated.
32 devices in a mesh: angle: 2 (over y), ty: 8 (over z, core), tx: 2 (over x).
Axes of the slice: x: 2, y: 2, z: 4, core: 2. Of those that a mesh axis runs over, the one named last changes fastest.
Arguments:
- object_slices: float32 [2, 2, 2048, 2048], P('angle', None, 'ty', 'tx'), may hold values from -5 to 5
- probe_field: float32 [2, 256, 256], replicated, may hold values from -6 to 6
- positions: int32 [2, 8, 2, 4, 2], P('angle', 'ty', 'tx'), may hold values from 0 to 1792, as said below
- live_slots: int32 [2, 8, 2], P('angle', 'ty', 'tx'), may hold values from 1 to 4, as said below
- photon_counts: int32 [2, 8, 2, 4, 256, 256], P('angle', 'ty', 'tx'), may hold values from 1 to 1600
Outputs:
- new_object: float32 [2, 2, 2048, 2048], P('angle', None, 'ty', 'tx')
- new_probe: float32 [2, 256, 256], P(None, 'ty')
Inputs may be any that keep to these rules, and one draw needn't show every extreme that they name: `positions`: A slot's patch lies inside the object and its centre (top-left plus 128) lies in the rows and columns of the tile that holds the slot: rows r * 256 to (r + 1) * 256 - 1, columns c * 1024 to (c + 1) * 1024 - 1. `live_slots`: some tile of every draw uses all 4 slots.
All inputs are finite; a program needn't handle non-finite values.
Results may differ from a plain program's by a relative error of at most 0.0003.
Values sent between devices are 32-bit elements; how exact they have to be, the bound alone decides.
A program may use at most 128 MiB of HBM per device.

v0:
```python
import functools
import math

import jax
import jax.numpy as jnp
import numpy as np
from jax import lax
from jax.experimental import pallas as pl
from jax.experimental.pallas import tpu as pltpu
from jax.sharding import PartitionSpec as P

MESH = pl.DeviceIdType.MESH
LANES = 128
VMEM_LIMIT = 56 * 1024 * 1024
AROUND = tuple((dy, dx) for dy in (-1, 0, 1) for dx in (-1, 0, 1))
BESIDE = tuple(d for d in AROUND if d != (0, 0))
DIAGONALS = tuple(d for d in BESIDE if d[0] and d[1])


def slot_of(dy, dx):
    return (dy + 1) * 3 + dx + 1


def present(dy, dx, shape):
    row = lax.axis_index("ty") + dy
    col = lax.axis_index("tx") + dx
    return (row >= 0) & (row < shape["ty"]) & (col >= 0) & (col < shape["tx"])


def beside_counts(shape):
    found = []
    for axis in ("ty", "tx"):
        at = lax.axis_index(axis)
        found.append(jnp.where(at > 0, 1, 0) + jnp.where(at < shape[axis] - 1, 1, 0))
    return found


def neighbour(dy, dx):
    return {"ty": lax.axis_index("ty") + dy, "tx": lax.axis_index("tx") + dx}


def edge_part(step, size, half):
    return {-1: (half, half), 0: (half, size), 1: (size, half)}[step]


def wide_part(step, size, half):
    return {-1: (0, half), 0: (half, size), 1: (half + size, half)}[step]


def region(ref, rows, blocks):
    return ref.at[:, pl.ds(*blocks), pl.ds(*rows), :]


def split(value):
    high = value.astype(jnp.bfloat16)
    low = (value - high.astype(jnp.float32)).astype(jnp.bfloat16)
    return high, low


def mm(a, b):
    return lax.dot_general(a, b, (((1,), (0,)), ((), ())), preferred_element_type=jnp.float32)


def cat(parts, axis):
    return jnp.concatenate(parts, axis=axis)


def step_kernel(
        shape, pos, live, tile_in, probe_in, counts_in, tables_in,
        out, out_probe,
        wide, tot, den, dbuf, metas, smetas, probe, counts, amp, tables, mats,
        sums, rim_v, rim_h, rim_c, r1, s1, r2, s2, r3, s3, g4, pk_own, pk_a, pk_b, pk_c,
        hsend, hrecv, nsend, nrecv, fsend, frecv, send1, recv1, send2, recv2, send3, recv3, send4, recv4,
        ksend, krecv, lsend, lrecv, msend, mrecv, local, local_tile):
    f32 = jnp.float32
    size = probe.shape[1]
    half = size // 2
    slots = counts.shape[0]
    rows, cols = tile_in.shape[1], tile_in.shape[2]
    inner = cols // LANES
    margin = half // LANES
    blocks = inner + 2 * margin
    pieces = size // LANES
    span = pieces + 1
    n_ty, n_tx, n_an = shape["ty"], shape["tx"], shape["angle"]
    ty, tx, an = lax.axis_index("ty"), lax.axis_index("tx"), lax.axis_index("angle")
    core, z = ty % 2, ty // 2
    n_z = n_ty // 2
    group = n_an * n_tx
    gid = an * n_tx + tx
    each = size // n_ty
    part = sums.shape[3] // n_an

    load_tile = [
        pltpu.make_async_copy(
            tile_in.at[:, :, pl.ds(j * LANES, LANES)],
            wide.at[:, margin + j, pl.ds(half, rows), :], local_tile.at[j])
        for j in range(inner)]
    load_probe = pltpu.make_async_copy(probe_in, probe, local.at[0])
    load_counts = [
        pltpu.make_async_copy(counts_in.at[:, :, pl.ds(b * LANES, LANES)], counts.at[:, b], local.at[4 + b])
        for b in range(pieces)]
    load_tables = pltpu.make_async_copy(tables_in, tables, local.at[2])
    for copy in load_tile + load_counts + [load_probe, load_tables]:
        copy.start()

    lane8 = lax.broadcasted_iota(jnp.int32, (8, LANES), 1)
    line = jnp.zeros((8, LANES), jnp.int32)
    for s in range(slots):
        line = jnp.where(lane8 == s, pos[0, s], line)
        line = jnp.where(lane8 == slots + s, pos[1, s], line)
    line = jnp.where(lane8 == 2 * slots, live[0], line)
    for k in range(9):
        metas[k] = line if k == 4 else jnp.zeros((8, LANES), jnp.int32)

    barrier = pltpu.get_barrier_semaphore()

    def signal(where):
        pl.semaphore_signal(barrier, inc=1, device_id=where, device_id_type=MESH)

    def member(d):
        g = (gid + d) % group
        return g, {"angle": g // n_tx, "tx": g % n_tx}

    for d in range(1, n_ty):
        signal({"ty": (ty + d) % n_ty})
    for d in range(1, group):
        signal(member(d)[1])
    for dy, dx in DIAGONALS:
        @pl.when(present(dy, dx, shape))
        def _():
            signal(neighbour(dy, dx))
    for copy in load_tile:
        copy.wait()
    n_row, n_col = beside_counts(shape)
    pl.semaphore_wait(barrier, n_ty - 1 + group - 1 + n_row * n_col)

    def rdma(src, dst, s_sem, r_sem, where):
        return pltpu.make_async_remote_copy(
            src_ref=src, dst_ref=dst, send_sem=s_sem, recv_sem=r_sem,
            device_id=where, device_id_type=MESH)

    def halo(dy, dx):
        k = slot_of(dy, dx)
        src = region(wide, edge_part(dy, rows, half), edge_part(dx, inner, margin))
        dst = region(wide, wide_part(-dy, rows, half), wide_part(-dx, inner, margin))
        return rdma(src, dst, hsend.at[k], hrecv.at[k], neighbour(dy, dx))

    def note(dy, dx):
        k = slot_of(dy, dx)
        return rdma(metas.at[4], metas.at[slot_of(-dy, -dx)], nsend.at[k], nrecv.at[k], neighbour(dy, dx))

    order = sorted(BESIDE, key=lambda d: abs(d[1]))
    for dy, dx in order:
        @pl.when(present(dy, dx, shape))
        def _():
            note(dy, dx).start()
    for dy, dx in order:
        @pl.when(present(dy, dx, shape))
        def _():
            halo(dy, dx).start()

    def landing(dy, dx):
        if dx == 0:
            return rim_v.at[(dy + 1) // 2]
        if dy == 0:
            return rim_h.at[(dx + 1) // 2]
        return rim_c.at[(dy + 1) + (dx + 1) // 2]

    for dy, dx in BESIDE:
        @pl.when(jnp.logical_not(present(dy, dx, shape)))
        def _():
            place = landing(-dy, -dx)
            place[...] = jnp.zeros(place.shape, f32)

    def clear(n, carry):
        s, ch = n // 2, n % 2
        tall = dbuf.shape[3]
        for b in (0, span + 1):
            dbuf[s, ch, b] = jnp.zeros((tall, LANES), f32)
        for b in range(1, span + 1):
            dbuf[s, ch, b, 0:size, :] = jnp.zeros((size, LANES), f32)
            dbuf[s, ch, b, 2 * size:, :] = jnp.zeros((tall - 2 * size, LANES), f32)
        return carry

    lax.fori_loop(0, 2 * slots, clear, 0)
    den[...] = jnp.zeros_like(den)
    sums[...] = jnp.zeros_like(sums)

    load_probe.wait()
    for dy, dx in order:
        @pl.when(present(dy, dx, shape))
        def _():
            note(dy, dx).wait_send()
            note(-dy, -dx).wait_recv()
    to_scalar = pltpu.make_async_copy(metas, smetas, local.at[3])
    to_scalar.start()
    to_scalar.wait()

    lane = lax.broadcasted_iota(jnp.int32, (size, LANES), 1)

    def spread(piece, shift):
        moved = [pltpu.roll(piece[:, b * LANES:(b + 1) * LANES], shift, axis=1) for b in range(pieces)]
        low = lane < shift
        found = [jnp.where(low, 0.0, moved[0])]
        for b in range(1, pieces):
            found.append(jnp.where(low, moved[b - 1], moved[b]))
        found.append(jnp.where(low, moved[-1], 0.0))
        return found

    def spot(k, s):
        return smetas[k, 0, s] - ty * rows + half, smetas[k, 0, slots + s] - tx * cols + half

    far = 64 * LANES

    def place(k, s):
        dy, dx = k // 3 - 1, k % 3 - 1
        row, at = spot(k, s)
        row = jnp.clip(row, dy * rows, dy * rows + rows - 1)
        at = jnp.clip(at, dx * cols, dx * cols + cols - 1)
        first = (at + far * LANES) // LANES - far
        return row, first, (at + far * LANES) % LANES

    power = probe[0] * probe[0] + probe[1] * probe[1]
    base = size

    def gathered(ch, j, start, count, spots):
        total = None
        for s, (row, first, _) in enumerate(spots):
            b = jnp.clip(j - first + 1, 0, span + 1)
            value = dbuf[s, ch, b, pl.ds(start - row + base, count), :]
            total = value if total is None else total + value
        return total

    chunk = half
    for k, (dy, dx) in enumerate(AROUND):
        there = present(dy, dx, shape)
        spots = [place(k, s) for s in range(slots)]

        def fill(s, carry):
            row, first, shift = place(k, s)
            used = there & (s < smetas[k, 0, 2 * slots])
            for b, value in enumerate(spread(jnp.where(used, power, 0.0), shift)):
                dbuf[s, 0, 1 + b, size:2 * size, :] = value
            return carry

        lax.fori_loop(0, slots, fill, 0)
        tall = range(0, rows, chunk) if dy == 0 else (range(0, half, chunk) if dy < 0 else range(rows - half, rows, chunk))
        if dx == 0:
            def column(j, carry):
                for r in tall:
                    den[j, r:r + chunk, :] += gathered(0, j + margin, half + r, chunk, spots)
                return carry

            lax.fori_loop(0, inner, column, 0)
        else:
            for j in range(margin) if dx < 0 else range(inner - margin, inner):
                for r in tall:
                    den[j, r:r + chunk, :] += gathered(0, j + margin, half + r, chunk, spots)

    def top(value):
        return jnp.max(jnp.max(value, axis=0, keepdims=True), axis=1, keepdims=True)

    pk_own[...] = jnp.broadcast_to(top(jnp.max(den[...], axis=0)), pk_own.shape)
    pk_a[pl.ds(gid, 1)] = pk_own[...][None]
    for d in range(1, group):
        g, where = member(d)
        rdma(pk_own, pk_a.at[gid], ksend.at[d], krecv.at[gid], where).start()

    load_tables.wait()
    for n in range(2):
        ce, se, co, so, cot, sot = [tables[6 * n + i] for i in range(6)]
        for m, (c, up, down) in enumerate(((ce, se, -se), (co, so, -so), (ce, -se, se), (cot, -sot, sot))):
            mats[n, m, 0:half, 0:half] = c
            mats[n, m, 0:half, half:] = up
            mats[n, m, half:, 0:half] = down
            mats[n, m, half:, half:] = c

    for copy in load_counts:
        copy.wait()
    from_lane = lax.broadcasted_iota(jnp.int32, (size, size), 0)
    to_lane = lax.broadcasted_iota(jnp.int32, (size, size), 1)
    wanted = jnp.where(to_lane < half, 2 * to_lane, 2 * (to_lane - half) + 1)
    shuffle = jnp.where(from_lane == wanted, 1.0, 0.0).astype(jnp.bfloat16)
    shuffle2 = cat([shuffle, shuffle], 0)

    def amplitude(s, carry):
        seen = cat([
            cat([counts[s, b, pl.ds(n, half, stride=2), :] for b in range(pieces)], 1) for n in range(2)], 0).astype(f32)
        amp[s] = 0.05 * jnp.sqrt(mm(cat(list(split(seen)), 1), shuffle2))
        return carry

    lax.fori_loop(0, slots, amplitude, 0)

    for d in range(1, group):
        g, where = member(d)
        rdma(pk_own, pk_a.at[g], ksend.at[d], krecv.at[g], where).wait()
    peak = pk_a[0]
    for g in range(1, group):
        peak = jnp.maximum(peak, pk_a[g])
    pk_b[pl.ds(ty, 1)] = peak[None]
    for d in range(1, n_ty):
        rdma(pk_b.at[ty], pk_b.at[ty], lsend.at[d], lrecv.at[ty], {"ty": (ty + d) % n_ty}).start()
    for d in range(1, n_ty):
        o = (ty + d) % n_ty
        rdma(pk_b.at[ty], pk_b.at[o], lsend.at[d], lrecv.at[o], {"ty": o}).wait()
    peak = pk_b[0]
    for t in range(1, n_ty):
        peak = jnp.maximum(peak, pk_b[t])
    den[...] = 1.0 / (den[...] + 0.1 * peak[0:1, 0:1])

    for dy, dx in order:
        @pl.when(present(dy, dx, shape))
        def _():
            halo(dy, dx).wait_send()
            halo(-dy, -dx).wait_recv()

    def matrix(m, axis):
        return cat([mats[0, m], mats[0, m], mats[1, m]], axis)

    def from_left(m, re, im):
        high, low = split(cat([re, im], 0))
        found = mm(matrix(m, 1), cat([high, low, high], 0))
        return found[:half], found[half:]

    def from_right(m, re, im):
        high, low = split(cat([re, im], 1))
        found = mm(cat([high, low, high], 1), matrix(m, 0))
        return found[:, :half], found[:, half:]

    def one_slot(s, carry):
        row, first, shift = place(4, s)
        used = s < smetas[4, 0, 2 * slots]
        back = (LANES - shift) % LANES
        keep = lane < LANES - shift

        def patch(ch):
            moved = [
                pltpu.roll(wide[ch, first + b, pl.ds(row, size), :], back, axis=1)
                for b in range(span)]
            return cat([jnp.where(keep, moved[b], moved[b + 1]) for b in range(pieces)], 1)

        x_re, x_im = patch(0), patch(1)
        q_re, q_im = probe[0], probe[1]
        p_re = q_re * x_re - q_im * x_im
        p_im = q_re * x_im + q_im * x_re
        a = from_left(0, p_re[:half] + p_re[half:], p_im[:half] + p_im[half:])
        b = from_left(1, p_re[:half] - p_re[half:], p_im[:half] - p_im[half:])
        y_re, y_im = cat([a[0], b[0]], 0), cat([a[1], b[1]], 0)
        a = from_right(2, y_re[:, :half] + y_re[:, half:], y_im[:, :half] + y_im[:, half:])
        b = from_right(3, y_re[:, :half] - y_re[:, half:], y_im[:, :half] - y_im[:, half:])
        f_re, f_im = cat([a[0], b[0]], 1), cat([a[1], b[1]], 1)
        factor = amp[s] * lax.rsqrt(jnp.maximum(f_re * f_re + f_im * f_im, 0.0625))
        g_re, g_im = f_re * factor, f_im * factor
        a = from_left(2, g_re[:half], g_im[:half])
        b = from_left(3, g_re[half:], g_im[half:])
        y_re, y_im = cat([a[0] + b[0], a[0] - b[0]], 0), cat([a[1] + b[1], a[1] - b[1]], 0)
        a = from_right(0, y_re[:, :half], y_im[:, :half])
        b = from_right(1, y_re[:, half:], y_im[:, half:])
        b_re, b_im = cat([a[0] + b[0], a[0] - b[0]], 1), cat([a[1] + b[1], a[1] - b[1]], 1)
        d_re, d_im = jnp.where(used, b_re - p_re, 0.0), jnp.where(used, b_im - p_im, 0.0)
        for ch, value in enumerate((q_re * d_re + q_im * d_im, q_re * d_im - q_im * d_re)):
            for i, moved in enumerate(spread(value, shift)):
                dbuf[s, ch, 1 + i, size:2 * size, :] = moved
        weighed = (
            x_re * d_re + x_im * d_im,
            x_re * d_im - x_im * d_re,
            jnp.where(used, x_re * x_re + x_im * x_im, 0.0))
        for t in range(n_ty):
            for ch in range(3):
                sums[t % 2, t // 2, ch * each:(ch + 1) * each, :] += weighed[ch][t * each:(t + 1) * each, :]
        return carry

    lax.fori_loop(0, slots, one_slot, 0)

    spots = [place(4, s) for s in range(slots)]
    pair = {"ty": ty + 1 - 2 * core}
    c1 = rdma(sums.at[1 - core], r1, send1.at[0], recv1.at[0], pair)
    c1.start()

    def total_at(start, count, lowest, number):
        def column(n, carry):
            j = lowest + n // 2
            ch = n % 2
            for r in range(start, start + count, chunk):
                tot[ch, j, r:r + chunk, :] = gathered(ch, j, r, chunk, spots)
            return carry

        lax.fori_loop(0, 2 * number, column, 0)

    total_at(0, half, 0, blocks)
    total_at(half + rows, half, 0, blocks)
    total_at(half, rows, 0, margin)
    total_at(half, rows, margin + inner, margin)

    early = half * 5 // 8 // 8 * 8

    def fold(dy, dx, piece=0):
        k = slot_of(dy, dx) + 9 * piece
        part_rows, part_cols = wide_part(dy, rows, half), wide_part(dx, inner, margin)
        place = landing(dy, dx)
        if dx == 0:
            begin, stop = (0, early) if piece == 0 else (early, half)
            part_rows = (part_rows[0] + begin, stop - begin)
            place = place.at[:, :, pl.ds(begin, stop - begin), :]
        return rdma(region(tot, part_rows, part_cols), place, fsend.at[k], frecv.at[k], neighbour(dy, dx))

    def start_folds(which):
        for dy, dx, piece in which:
            @pl.when(present(dy, dx, shape))
            def _():
                fold(dy, dx, piece).start()

    start_folds([(-1, 0, 0), (1, 0, 0), (0, -1, 0), (0, 1, 0)])

    c1.wait()
    s1[...] = sums[core] + r1[...]

    def lanes(ref, a):
        return ref.at[:, :, pl.ds(pl.multiple_of(a * part, part), part)]

    for d in range(1, n_an):
        a = (an + d) % n_an
        rdma(lanes(s1, a), r2.at[an], send2.at[d], recv2.at[an], {"angle": a}).start()

    def centre_column(j, carry):
        for ch in range(2):
            for r in range(half, half + rows, chunk):
                tot[ch, j + margin, r:r + chunk, :] = gathered(ch, j + margin, r, chunk, spots)
        return carry

    lax.fori_loop(0, inner, centre_column, 0)

    for d in range(1, n_an):
        a = (an + d) % n_an
        rdma(lanes(s1, a), r2.at[a], send2.at[d], recv2.at[a], {"angle": a}).wait()
    mine = s1[:, :, pl.ds(pl.multiple_of(an * part, part), part)]
    for d in range(1, n_an):
        mine = mine + r2[(an + d) % n_an]
    s2[...] = mine

    for d in range(1, n_z):
        o = (z + d) % n_z
        rdma(s2.at[o], r3.at[z], send3.at[d], recv3.at[z], {"ty": o * 2 + core}).start()
    start_folds([(-1, 0, 1), (1, 0, 1)] + [(dy, dx, 0) for dy, dx in DIAGONALS])
    for d in range(1, n_z):
        o = (z + d) % n_z
        rdma(s2.at[o], r3.at[o], send3.at[d], recv3.at[o], {"ty": o * 2 + core}).wait()
    total = s2[z]
    for d in range(1, n_z):
        total = total + r3[(z + d) % n_z]
    s3[...] = total
    g4[pl.ds(gid, 1)] = total[None]

    for d in range(1, group):
        g, where = member(d)
        rdma(s3, g4.at[gid], send4.at[d], recv4.at[gid], where).start()
    for d in range(1, group):
        g, where = member(d)
        rdma(s3, g4.at[g], send4.at[d], recv4.at[g], where).wait()
    found = []
    for a in range(n_an):
        piece = g4[a * n_tx]
        for t in range(1, n_tx):
            piece = piece + g4[a * n_tx + t]
        found.append(piece)
    full = cat(found, 1)
    p_re, p_im, p_den = full[:each], full[each:2 * each], full[2 * each:]

    pk_c[pl.ds(ty, 1)] = jnp.broadcast_to(top(p_den), pk_own.shape)[None]
    for d in range(1, n_ty):
        rdma(pk_c.at[ty], pk_c.at[ty], msend.at[d], mrecv.at[ty], {"ty": (ty + d) % n_ty}).start()

    for dy, dx in BESIDE:
        @pl.when(present(dy, dx, shape))
        def _():
            for piece in (0, 1) if dx == 0 else (0,):
                fold(dy, dx, piece).wait_send()
                fold(-dy, -dx, piece).wait_recv()

    def final(ch, j, extra):
        for r in range(0, rows, chunk):
            value = tot[ch, j + margin, half + r:half + r + chunk, :]
            for r_from, c_from, found in extra:
                if r_from == 0 or (r_from < 0 and r < half) or (r_from > 0 and r >= rows - half):
                    at = r if r_from <= 0 else r - (rows - half)
                    value = value + found(ch, j, at)
            own = wide[ch, j + margin, half + r:half + r + chunk, :]
            yield r, own + value * den[j, r:r + chunk, :]

    def from_rim(dy, dx):
        place = landing(-dy, -dx)
        lowest = inner - margin if dx > 0 else 0
        return dy, dx, lambda ch, j, at: place[ch, j - lowest, at:at + chunk, :]

    for j in range(inner):
        here = [(-1, 0), (1, 0)]
        if j < margin:
            here += [(dy, -1) for dy in (-1, 0, 1)]
        if j >= inner - margin:
            here += [(dy, 1) for dy in (-1, 0, 1)]
        for ch in range(2):
            for r, value in final(ch, j, [from_rim(dy, dx) for dy, dx in here]):
                out[ch, r:r + chunk, j * LANES:(j + 1) * LANES] = value

    for d in range(1, n_ty):
        o = (ty + d) % n_ty
        rdma(pk_c.at[ty], pk_c.at[o], msend.at[d], mrecv.at[o], {"ty": o}).wait()
    peak = pk_c[0]
    for t in range(1, n_ty):
        peak = jnp.maximum(peak, pk_c[t])
    scale = 1.0 / (p_den + 0.1 * peak[0:1, 0:1])
    own_rows = pl.ds(pl.multiple_of(ty * each, each), each)
    out_probe[0] = probe[0, own_rows, :] + p_re * scale
    out_probe[1] = probe[1, own_rows, :] + p_im * scale


def table_values(length):
    half = length // 2
    j, m = np.arange(half), np.arange(half)
    even = 2.0 * math.pi / length * (np.outer(2 * m, j) % length)
    odd = 2.0 * math.pi / length * (np.outer(2 * m + 1, j) % length)
    values = []
    for phase in (even, odd, odd.T):
        values += [np.cos(phase) / math.sqrt(length), np.sin(phase) / math.sqrt(length)]
    high = [value.astype(jnp.bfloat16) for value in values]
    low = [(value - h.astype(np.float64)).astype(jnp.bfloat16) for value, h in zip(values, high)]
    return np.stack(high + low)


def body(shape, object_slices, probe_field, positions, live_slots, photon_counts):
    f32 = jnp.float32
    dma = pltpu.SemaphoreType.DMA
    size = probe_field.shape[1]
    half = size // 2
    tile = object_slices[0]
    _, rows, cols = tile.shape
    spots = positions[0, 0, 0].T
    slots = spots.shape[1]
    inner, margin = cols // LANES, half // LANES
    blocks = inner + 2 * margin
    span = size // LANES + 1
    n_ty, n_tx, n_an = shape["ty"], shape["tx"], shape["angle"]
    n_z, each, group = n_ty // 2, size // n_ty, n_an * n_tx
    part = size // n_an
    vmem = pl.BlockSpec(memory_space=pltpu.VMEM)
    smem = pl.BlockSpec(memory_space=pltpu.SMEM)
    hbm = pl.BlockSpec(memory_space=pltpu.HBM)

    return pl.pallas_call(
        functools.partial(step_kernel, shape),
        out_shape=(
            jax.ShapeDtypeStruct((2, rows, cols), f32),
            jax.ShapeDtypeStruct((2, each, size), f32),
        ),
        in_specs=[smem, smem, hbm, hbm, hbm, hbm],
        out_specs=(vmem, vmem),
        scratch_shapes=[
            pltpu.VMEM((2, blocks, rows + size, LANES), f32),
            pltpu.VMEM((2, blocks, rows + size, LANES), f32),
            pltpu.VMEM((inner, rows, LANES), f32),
            pltpu.VMEM((slots, 2, span + 2, rows + 2 * size, LANES), f32),
            pltpu.VMEM((9, 8, LANES), jnp.int32),
            pltpu.SMEM((9, 8, LANES), jnp.int32),
            pltpu.VMEM((2, size, size), f32),
            pltpu.VMEM((slots, size // LANES, size, LANES), jnp.int32),
            pltpu.VMEM((slots, size, size), f32),
            pltpu.VMEM((12, half, half), jnp.bfloat16),
            pltpu.VMEM((2, 4, size, size), jnp.bfloat16),
            pltpu.VMEM((2, n_z, 3 * each, size), f32),
            pltpu.VMEM((2, 2, inner, half, LANES), f32),
            pltpu.VMEM((2, 2, margin, rows, LANES), f32),
            pltpu.VMEM((4, 2, margin, half, LANES), f32),
            pltpu.VMEM((n_z, 3 * each, size), f32),
            pltpu.VMEM((n_z, 3 * each, size), f32),
            pltpu.VMEM((n_an, n_z, 3 * each, part), f32),
            pltpu.VMEM((n_z, 3 * each, part), f32),
            pltpu.VMEM((n_z, 3 * each, part), f32),
            pltpu.VMEM((3 * each, part), f32),
            pltpu.VMEM((group, 3 * each, part), f32),
            pltpu.VMEM((8, LANES), f32),
            pltpu.VMEM((group, 8, LANES), f32),
            pltpu.VMEM((n_ty, 8, LANES), f32),
            pltpu.VMEM((n_ty, 8, LANES), f32),
            dma((9,)), dma((9,)), dma((9,)), dma((9,)),
            dma((18,)), dma((18,)), dma((1,)), dma((1,)), dma((n_an,)), dma((n_an,)),
            dma((n_z,)), dma((n_z,)), dma((group,)), dma((group,)),
            dma((group,)), dma((group,)), dma((n_ty,)), dma((n_ty,)), dma((n_ty,)), dma((n_ty,)),
            dma((4 + size // LANES,)), dma((inner,)),
        ],
        compiler_params=pltpu.CompilerParams(
            collective_id=0, has_side_effects=True, vmem_limit_bytes=VMEM_LIMIT),
    )(spots, live_slots[0, 0], tile, probe_field, photon_counts[0, 0, 0], jnp.asarray(table_values(size)))


def solution(mesh):
    shape = dict(mesh.shape)

    def step(*args):
        new_tile, new_probe = body(shape, *args)
        return new_tile[None], new_probe

    return jax.shard_map(
        step,
        mesh=mesh,
        in_specs=(
            P("angle", None, "ty", "tx"),
            P(),
            P("angle", "ty", "tx", None, None),
            P("angle", "ty", "tx"),
            P("angle", "ty", "tx", None, None, None),
        ),
        out_specs=(P("angle", None, "ty", "tx"), P(None, "ty", None)),
        check_vma=False,
    )
```

profile of v0, /device:TPU:1, one launch (start us, length us, event | category | flops | bytes accessed | tf_op | source)
XLA Modules:
  0.0 63.2 jit_solution(10910718449486471721)
XLA Ops:
  1.3 58.1 %shard_map.77 = (f32[2,256,1024]{2,1,0:T(8,128)}, f32[2,32,256]{2,1,0:T(8,128)}) custom-call(s32[2,4]{1,0:T(2,128)} %bitcast.11, s32[1]{0:T(128)} %bitcast.7.live, f32[2,256,1024]{2,1,0:T(8,128)} %bitcast.8, f32[2,256,256]{2,1,0:T(8,128)} %probe_in.1, s32[4,256,256]{2,1,0:T(8,128)} %bitcast.10, bf16[12,128,128]{2,1,0:T(8,128)(2,1)} %constant.2.clone.tables_in), custom_call_target="tpu_custom_call" | custom-call | tf_op jit(solution)/shard_map/pallas_call | solution.py:550
  59.4 0.0 copy-start
  59.4 3.2 %copy.11 = f32[1,2,256,1024]{3,2,1,0:T(8,128)} copy(f32[1,2,256,1024]{3,2,1,0:T(8,128)} %bitcast.9) | data formatting | bytes 4194304
  62.6 0.0 copy-done
  62.6 0.6 copy.12
Async XLA Ops:
  59.4 3.2 %copy-start = (f32[2,32,256]{2,1,0:T(8,128)S(1)}, f32[2,32,256]{2,1,0:T(8,128)}, u32[]{:S(2)}) copy-start(f32[2,32,256]{2,1,0:T(8,128)} %get-tuple-element.9) | copy-start | bytes 196612
where the time goes:
time: 63.7 us; the launch traced here: 63.2 us
  Pallas kernels  58.1 us (91%)
  local copies, waits for them, and re-layouts  3.82 us (6%)
  between operations  1.29 us (2%)
    pallas_call x1, Pallas kernels, body(): pl.pallas_call(functools.partial(step_kernel, shape), out_shape=(jax.Shap...  58.1 us
    unnamed x4, local copies, waits for them, and re-layouts  3.82 us

commit v1 on v0

v1 whole, which is shorter than its diff:
```python
import functools
import math

import jax
import jax.numpy as jnp
import numpy as np
from jax import lax
from jax.experimental import pallas as pl
from jax.experimental.pallas import tpu as pltpu
from jax.sharding import PartitionSpec as P

MESH = pl.DeviceIdType.MESH
LANES = 128
VMEM_LIMIT = 44 * 1024 * 1024
FINISH_LIMIT = 4 * 1024 * 1024
AROUND = tuple((dy, dx) for dy in (-1, 0, 1) for dx in (-1, 0, 1))
BESIDE = tuple(d for d in AROUND if d != (0, 0))
DIAGONALS = tuple(d for d in BESIDE if d[0] and d[1])


def slot_of(dy, dx):
    return (dy + 1) * 3 + dx + 1


def present(dy, dx, shape):
    row = lax.axis_index("ty") + dy
    col = lax.axis_index("tx") + dx
    return (row >= 0) & (row < shape["ty"]) & (col >= 0) & (col < shape["tx"])


def beside_counts(shape):
    found = []
    for axis in ("ty", "tx"):
        at = lax.axis_index(axis)
        found.append(jnp.where(at > 0, 1, 0) + jnp.where(at < shape[axis] - 1, 1, 0))
    return found


def neighbour(dy, dx):
    return {"ty": lax.axis_index("ty") + dy, "tx": lax.axis_index("tx") + dx}


def edge_part(step, size, half):
    return {-1: (half, half), 0: (half, size), 1: (size, half)}[step]


def wide_part(step, size, half):
    return {-1: (0, half), 0: (half, size), 1: (half + size, half)}[step]


def region(ref, rows, blocks):
    return ref.at[:, pl.ds(*blocks), pl.ds(*rows), :]


def split(value):
    high = value.astype(jnp.bfloat16)
    low = (value - high.astype(jnp.float32)).astype(jnp.bfloat16)
    return high, low


def mm(a, b):
    return lax.dot_general(a, b, (((1,), (0,)), ((), ())), preferred_element_type=jnp.float32)


def cat(parts, axis):
    return jnp.concatenate(parts, axis=axis)


def step_kernel(
        shape, live, pos_in, tile_in, probe_in, counts_in, tables_in,
        out, out_probe,
        pos, wide, tot, den, dbuf, metas, smetas, probe, counts, amp, tables, mats,
        xbuf, rim_v, rim_h, pk_own, pk_a, pk_b, pk_c,
        hsend, hrecv, nsend, nrecv, fsend, frecv, ksend, krecv, lsend, lrecv, msend, mrecv, local, local_tile,
        *chain_refs):
    f32 = jnp.float32
    size = probe.shape[1]
    half = size // 2
    slots = counts.shape[0]
    rows, cols = tile_in.shape[1], tile_in.shape[2]
    inner = cols // LANES
    margin = half // LANES
    blocks = inner + 2 * margin
    pieces = size // LANES
    span = pieces + 1
    n_ty, n_tx, n_an = shape["ty"], shape["tx"], shape["angle"]
    ty, tx, an = lax.axis_index("ty"), lax.axis_index("tx"), lax.axis_index("angle")
    core, z = ty % 2, ty // 2
    n_z = n_ty // 2
    group = n_an * n_tx
    gid = an * n_tx + tx
    each = size // n_ty
    part = size // n_an
    den_refs, num_refs = chain_refs[:len(chain_refs) // 2], chain_refs[len(chain_refs) // 2:]
    sums_d, sums_n = den_refs[0], num_refs[0]

    load_pos = pltpu.make_async_copy(pos_in, pos, local.at[3])
    load_pos.start()
    load_tile = [
        pltpu.make_async_copy(
            tile_in.at[:, :, pl.ds(j * LANES, LANES)],
            wide.at[:, margin + j, pl.ds(half, rows), :], local_tile.at[j])
        for j in range(inner)]
    load_probe = pltpu.make_async_copy(probe_in, probe, local.at[0])
    load_counts = [
        pltpu.make_async_copy(counts_in.at[:, :, pl.ds(b * LANES, LANES)], counts.at[:, b], local.at[4 + b])
        for b in range(pieces)]
    load_tables = pltpu.make_async_copy(tables_in, tables, local.at[2])
    for copy in load_tile + load_counts + [load_probe, load_tables]:
        copy.start()

    load_pos.wait()
    lane8 = lax.broadcasted_iota(jnp.int32, (8, LANES), 1)
    line = jnp.zeros((8, LANES), jnp.int32)
    for s in range(slots):
        line = jnp.where(lane8 == s, pos[0, s], line)
        line = jnp.where(lane8 == slots + s, pos[1, s], line)
    line = jnp.where(lane8 == 2 * slots, live[0, 0], line)
    for k in range(9):
        metas[k] = line if k == 4 else jnp.zeros((8, LANES), jnp.int32)

    barrier = pltpu.get_barrier_semaphore()

    def signal(where):
        pl.semaphore_signal(barrier, inc=1, device_id=where, device_id_type=MESH)

    def member(d):
        g = (gid + d) % group
        return g, {"angle": g // n_tx, "tx": g % n_tx}

    for d in range(1, n_ty):
        signal({"ty": (ty + d) % n_ty})
    for d in range(1, group):
        signal(member(d)[1])
    for dy, dx in DIAGONALS:
        @pl.when(present(dy, dx, shape))
        def _():
            signal(neighbour(dy, dx))
    def landing(dy, dx):
        return rim_v.at[(dy + 1) // 2] if dx == 0 else rim_h.at[(dx + 1) // 2]

    for dy, dx in ((-1, 0), (1, 0), (0, -1), (0, 1)):
        @pl.when(jnp.logical_not(present(dy, dx, shape)))
        def _():
            place = landing(-dy, -dx)
            place[...] = jnp.zeros(place.shape, f32)

    for dy, dx in BESIDE:
        @pl.when(jnp.logical_not(present(dy, dx, shape)))
        def _():
            place = landing(-dy, -dx)
            place[...] = jnp.zeros(place.shape, f32)

    def clear(n, carry):
        s, ch = n // 2, n % 2
        tall = dbuf.shape[3]
        for b in (0, span + 1):
            dbuf[s, ch, b] = jnp.zeros((tall, LANES), f32)
        for b in range(1, span + 1):
            dbuf[s, ch, b, 0:size, :] = jnp.zeros((size, LANES), f32)
            dbuf[s, ch, b, 2 * size:, :] = jnp.zeros((tall - 2 * size, LANES), f32)
        return carry

    lax.fori_loop(0, 2 * slots, clear, 0)
    den[...] = jnp.zeros_like(den)
    sums_d[...] = jnp.zeros_like(sums_d)
    sums_n[...] = jnp.zeros_like(sums_n)

    load_tables.wait()
    for n in range(2):
        ce, se, co, so, cot, sot = [tables[6 * n + i] for i in range(6)]
        for m, (c, up, down) in enumerate(((ce, se, -se), (co, so, -so), (ce, -se, se), (cot, -sot, sot))):
            mats[n, m, 0:half, 0:half] = c
            mats[n, m, 0:half, half:] = up
            mats[n, m, half:, 0:half] = down
            mats[n, m, half:, half:] = c

    for copy in load_tile:
        copy.wait()
    n_row, n_col = beside_counts(shape)
    pl.semaphore_wait(barrier, n_ty - 1 + group - 1 + n_row * n_col)

    def rdma(src, dst, s_sem, r_sem, where):
        return pltpu.make_async_remote_copy(
            src_ref=src, dst_ref=dst, send_sem=s_sem, recv_sem=r_sem,
            device_id=where, device_id_type=MESH)

    strips = ((margin, margin), (inner, margin), (2 * margin, inner - 2 * margin))
    SIDES = ((-1, 0), (1, 0), (0, -1), (0, 1))

    def halo_v(dy, i):
        src = region(wide, edge_part(dy, rows, half), strips[i])
        dst = region(wide, wide_part(-dy, rows, half), strips[i])
        k = (dy + 1) // 2 * len(strips) + i
        return rdma(src, dst, hsend.at[k], hrecv.at[k], neighbour(dy, 0))

    def halo_h(dx, dy):
        part_rows = wide_part(dy, rows, half)
        src = region(wide, part_rows, edge_part(dx, inner, margin))
        dst = region(wide, part_rows, wide_part(-dx, inner, margin))
        k = 2 * len(strips) + (dx + 1) // 2 * 3 + dy + 1
        return rdma(src, dst, hsend.at[k], hrecv.at[k], neighbour(0, dx))

    def note(dy, dx):
        k = slot_of(dy, dx)
        return rdma(metas.at[4], metas.at[slot_of(-dy, -dx)], nsend.at[k], nrecv.at[k], neighbour(dy, dx))

    order = sorted(BESIDE, key=lambda d: abs(d[1]))
    for dy, dx in order:
        @pl.when(present(dy, dx, shape))
        def _():
            note(dy, dx).start()
    for dy, dx in SIDES:
        @pl.when(present(dy, dx, shape))
        def _():
            if dx == 0:
                halo_v(dy, 0).start()
                halo_v(dy, 1).start()
            else:
                halo_h(dx, 0).start()
    for dy in (-1, 1):
        @pl.when(present(dy, 0, shape))
        def _():
            halo_v(dy, 2).start()

    for copy in load_counts:
        copy.wait()
    from_lane = lax.broadcasted_iota(jnp.int32, (size, size), 0)
    to_lane = lax.broadcasted_iota(jnp.int32, (size, size), 1)
    wanted = jnp.where(to_lane < half, 2 * to_lane, 2 * (to_lane - half) + 1)
    shuffle = jnp.where(from_lane == wanted, 1.0, 0.0).astype(jnp.bfloat16)
    shuffle2 = cat([shuffle, shuffle], 0)

    def amplitude(s, carry):
        seen = cat([
            cat([counts[s, b, pl.ds(n, half, stride=2), :] for b in range(pieces)], 1) for n in range(2)], 0).astype(f32)
        amp[s] = 0.05 * jnp.sqrt(mm(cat(list(split(seen)), 1), shuffle2))
        return carry

    lax.fori_loop(0, slots, amplitude, 0)

    load_probe.wait()
    for dy, dx in order:
        @pl.when(present(dy, dx, shape))
        def _():
            note(dy, dx).wait_send()
            note(-dy, -dx).wait_recv()
    for dy in (-1, 1):
        @pl.when(present(dy, 0, shape))
        def _():
            halo_v(-dy, 0).wait_recv()
            halo_v(-dy, 1).wait_recv()
    for dy, dx in DIAGONALS:
        @pl.when(present(dy, dx, shape))
        def _():
            halo_h(dx, dy).start()
    to_scalar = pltpu.make_async_copy(metas, smetas, local.at[3])
    to_scalar.start()
    to_scalar.wait()

    lane = lax.broadcasted_iota(jnp.int32, (size, LANES), 1)

    def spread(piece, shift):
        moved = [pltpu.roll(piece[:, b * LANES:(b + 1) * LANES], shift, axis=1) for b in range(pieces)]
        low = lane[:piece.shape[0]] < shift
        found = [jnp.where(low, 0.0, moved[0])]
        for b in range(1, pieces):
            found.append(jnp.where(low, moved[b - 1], moved[b]))
        found.append(jnp.where(low, moved[-1], 0.0))
        return found

    def spot(k, s):
        return smetas[k, 0, s] - ty * rows + half, smetas[k, 0, slots + s] - tx * cols + half

    far = 64 * LANES

    def place(k, s):
        dy, dx = k // 3 - 1, k % 3 - 1
        row, at = spot(k, s)
        row = jnp.clip(row, dy * rows, dy * rows + rows - 1)
        at = jnp.clip(at, dx * cols, dx * cols + cols - 1)
        first = (at + far * LANES) // LANES - far
        return row, first, (at + far * LANES) % LANES

    power = probe[0] * probe[0] + probe[1] * probe[1]
    base = size

    def gathered(ch, j, start, count, spots):
        total = None
        for s, (row, first, _) in enumerate(spots):
            b = jnp.clip(j - first + 1, 0, span + 1)
            value = dbuf[s, ch, b, pl.ds(start - row + base, count), :]
            total = value if total is None else total + value
        return total

    chunk = half
    for k, (dy, dx) in enumerate(AROUND):
        there = present(dy, dx, shape)
        spots = [place(k, s) for s in range(slots)]

        part_rows = {-1: (half, size), 0: (0, size), 1: (0, half)}[dy]
        for s in range(slots):
            used = there & (s < smetas[k, 0, 2 * slots])
            piece = jnp.where(used, power[part_rows[0]:part_rows[1]], 0.0)
            for b, value in enumerate(spread(piece, spots[s][2])):
                dbuf[s, 0, 1 + b, size + part_rows[0]:size + part_rows[1], :] = value
        tall = range(0, rows, chunk) if dy == 0 else (range(0, half, chunk) if dy < 0 else range(rows - half, rows, chunk))
        if dx == 0:
            def column(j, carry):
                for r in tall:
                    den[j, r:r + chunk, :] += gathered(0, j + margin, half + r, chunk, spots)
                return carry

            lax.fori_loop(0, inner, column, 0)
        else:
            for j in range(margin) if dx < 0 else range(inner - margin, inner):
                for r in tall:
                    den[j, r:r + chunk, :] += gathered(0, j + margin, half + r, chunk, spots)

    def top(value):
        return jnp.max(jnp.max(value, axis=0, keepdims=True), axis=1, keepdims=True)

    pk_own[...] = jnp.broadcast_to(top(jnp.max(den[...], axis=0)), pk_own.shape)
    pk_a[pl.ds(gid, 1)] = pk_own[...][None]
    for d in range(1, group):
        g, where = member(d)
        rdma(pk_own, pk_a.at[gid], ksend.at[d], krecv.at[gid], where).start()

    for dy, dx in SIDES:
        @pl.when(present(dy, dx, shape))
        def _():
            if dx == 0:
                for i in range(len(strips)):
                    halo_v(dy, i).wait_send()
                halo_v(-dy, 2).wait_recv()
            else:
                halo_h(dx, 0).wait_send()
                halo_h(-dx, 0).wait_recv()
    for dy, dx in DIAGONALS:
        @pl.when(present(dy, dx, shape))
        def _():
            halo_h(dx, dy).wait_send()
            halo_h(-dx, dy).wait_recv()

    def matrix(m, axis):
        return cat([mats[0, m], mats[0, m], mats[1, m]], axis)

    def from_left(m, re, im):
        high, low = split(cat([re, im], 0))
        found = mm(matrix(m, 1), cat([high, low, high], 0))
        return found[:half], found[half:]

    def from_right(m, re, im):
        high, low = split(cat([re, im], 1))
        found = mm(cat([high, low, high], 1), matrix(m, 0))
        return found[:, :half], found[:, half:]

    def add_to(total, s, values):
        for t in range(n_ty):
            for ch, value in enumerate(values):
                total[t % 2, t // 2, ch * each:(ch + 1) * each, :] += value[t * each:(t + 1) * each, :]

    def extract(s, carry):
        row, first, shift = place(4, s)
        used = s < smetas[4, 0, 2 * slots]
        back = (LANES - shift) % LANES
        keep = lane < LANES - shift
        found = []
        for ch in range(2):
            moved = [
                pltpu.roll(wide[ch, first + b, pl.ds(row, size), :], back, axis=1)
                for b in range(span)]
            found.append(cat([jnp.where(keep, moved[b], moved[b + 1]) for b in range(pieces)], 1))
            xbuf[s, ch] = found[ch]
        add_to(sums_d, s, (jnp.where(used, found[0] * found[0] + found[1] * found[1], 0.0),))
        return carry

    def one_slot(s, carry):
        shift = place(4, s)[2]
        used = s < smetas[4, 0, 2 * slots]
        x_re, x_im = xbuf[s, 0], xbuf[s, 1]
        q_re, q_im = probe[0], probe[1]
        p_re = q_re * x_re - q_im * x_im
        p_im = q_re * x_im + q_im * x_re
        a = from_left(0, p_re[:half] + p_re[half:], p_im[:half] + p_im[half:])
        b = from_left(1, p_re[:half] - p_re[half:], p_im[:half] - p_im[half:])
        y_re, y_im = cat([a[0], b[0]], 0), cat([a[1], b[1]], 0)
        a = from_right(2, y_re[:, :half] + y_re[:, half:], y_im[:, :half] + y_im[:, half:])
        b = from_right(3, y_re[:, :half] - y_re[:, half:], y_im[:, :half] - y_im[:, half:])
        f_re, f_im = cat([a[0], b[0]], 1), cat([a[1], b[1]], 1)
        factor = amp[s] * lax.rsqrt(jnp.maximum(f_re * f_re + f_im * f_im, 0.0625))
        g_re, g_im = f_re * factor, f_im * factor
        a = from_left(2, g_re[:half], g_im[:half])
        b = from_left(3, g_re[half:], g_im[half:])
        y_re, y_im = cat([a[0] + b[0], a[0] - b[0]], 0), cat([a[1] + b[1], a[1] - b[1]], 0)
        a = from_right(0, y_re[:, :half], y_im[:, :half])
        b = from_right(1, y_re[:, half:], y_im[:, half:])
        b_re, b_im = cat([a[0] + b[0], a[0] - b[0]], 1), cat([a[1] + b[1], a[1] - b[1]], 1)
        d_re, d_im = jnp.where(used, b_re - p_re, 0.0), jnp.where(used, b_im - p_im, 0.0)
        for ch, value in enumerate((q_re * d_re + q_im * d_im, q_re * d_im - q_im * d_re)):
            for i, moved in enumerate(spread(value, shift)):
                dbuf[s, ch, 1 + i, size:2 * size, :] = moved
        add_to(sums_n, s, (x_re * d_re + x_im * d_im, x_re * d_im - x_im * d_re))
        return carry

    def lanes(ref, a):
        return ref.at[:, :, pl.ds(pl.multiple_of(a * part, part), part)]

    class Chain:
        def __init__(self, refs):
            (self.sums, self.r1, self.s1, self.r2, self.s2, self.r3, self.s3, self.g4,
             self.send1, self.recv1, self.send2, self.recv2, self.send3, self.recv3, self.send4, self.recv4) = refs

        def pair(self):
            return rdma(self.sums.at[1 - core], self.r1, self.send1.at[0], self.recv1.at[0], {"ty": ty + 1 - 2 * core})

        def over_angle(self, d, get):
            a = (an + d) % n_an
            return rdma(
                lanes(self.s1, a), self.r2.at[a if get else an], self.send2.at[d],
                self.recv2.at[a if get else an], {"angle": a})

        def over_z(self, d, get):
            o = (z + d) % n_z
            return rdma(
                self.s2.at[o], self.r3.at[o if get else z], self.send3.at[d],
                self.recv3.at[o if get else z], {"ty": o * 2 + core})

        def over_group(self, d, get):
            g, where = member(d)
            at = g if get else gid
            return rdma(self.s3, self.g4.at[at], self.send4.at[d], self.recv4.at[at], where)

        def step1(self):
            self.pair().start()

        def step2(self):
            self.pair().wait()
            self.s1[...] = self.sums[core] + self.r1[...]
            for d in range(1, n_an):
                self.over_angle(d, False).start()

        def step3(self):
            for d in range(1, n_an):
                self.over_angle(d, True).wait()
            total = self.s1[:, :, pl.ds(pl.multiple_of(an * part, part), part)]
            for d in range(1, n_an):
                total = total + self.r2[(an + d) % n_an]
            self.s2[...] = total
            for d in range(1, n_z):
                self.over_z(d, False).start()

        def step4(self):
            for d in range(1, n_z):
                self.over_z(d, True).wait()
            total = self.s2[z]
            for d in range(1, n_z):
                total = total + self.r3[(z + d) % n_z]
            self.s3[...] = total
            self.g4[pl.ds(gid, 1)] = total[None]
            for d in range(1, group):
                self.over_group(d, False).start()

        def result(self):
            for d in range(1, group):
                self.over_group(d, True).wait()
            found = []
            for a in range(n_an):
                piece = self.g4[a * n_tx]
                for t in range(1, n_tx):
                    piece = piece + self.g4[a * n_tx + t]
                found.append(piece)
            return cat(found, 1)

    den_chain, num_chain = Chain(den_refs), Chain(num_refs)
    def some_slots(*which):
        for s in which:
            one_slot(s, 0)

    lax.fori_loop(0, slots, extract, 0)
    den_chain.step1()
    some_slots(0)
    den_chain.step2()
    some_slots(*range(1, slots - 1))
    den_chain.step3()
    some_slots(slots - 1)
    num_chain.step1()

    for d in range(1, group):
        g, where = member(d)
        rdma(pk_own, pk_a.at[g], ksend.at[d], krecv.at[g], where).wait()
    peak = pk_a[0]
    for g in range(1, group):
        peak = jnp.maximum(peak, pk_a[g])
    pk_b[pl.ds(ty, 1)] = peak[None]
    for d in range(1, n_ty):
        rdma(pk_b.at[ty], pk_b.at[ty], lsend.at[d], lrecv.at[ty], {"ty": (ty + d) % n_ty}).start()
    spots = [place(4, s) for s in range(slots)]
    def total_at(start, count, lowest, number):
        def column(n, carry):
            j = lowest + n // 2
            ch = n % 2
            for r in range(start, start + count, chunk):
                tot[ch, j, r:r + chunk, :] = gathered(ch, j, r, chunk, spots)
            return carry

        lax.fori_loop(0, 2 * number, column, 0)

    def fold_h(dx, dy):
        part_rows = wide_part(dy, rows, half)
        k = (dx + 1) // 2 * 3 + dy + 1
        return rdma(
            region(tot, part_rows, wide_part(dx, inner, margin)),
            landing(0, dx).at[:, :, pl.ds(*part_rows), :], fsend.at[k], frecv.at[k], neighbour(0, dx))

    middle = inner - 2 * margin
    first = middle * 2 // 3
    groups = ((2 * margin, first), (2 * margin + first, middle - first), (margin, margin), (inner, margin))

    def fold_v(dy, i):
        start, count = groups[i]
        k = 6 + (dy + 1) // 2 * len(groups) + i
        return rdma(
            region(tot, wide_part(dy, rows, half), groups[i]),
            landing(dy, 0).at[:, pl.ds(start - margin, count)], fsend.at[k], frecv.at[k], neighbour(dy, 0))

    def start_folds_v(which):
        for dy in (-1, 1):
            @pl.when(present(dy, 0, shape))
            def _():
                for i in which:
                    fold_v(dy, i).start()

    def start_folds_h(which):
        for dx in (-1, 1):
            @pl.when(present(0, dx, shape))
            def _():
                for dy in which:
                    fold_h(dx, dy).start()

    total_at(0, half, margin, inner)
    total_at(half + rows, half, margin, inner)
    start_folds_v((0,))
    total_at(0, 2 * half + rows, 0, margin)
    total_at(0, 2 * half + rows, margin + inner, margin)
    start_folds_h((-1,))
    num_chain.step2()
    total_at(half, rows, margin, inner)
    den_chain.step4()
    start_folds_h((1, 0))
    num_chain.step3()
    start_folds_v((1,))
    p_den = den_chain.result()
    pk_c[pl.ds(ty, 1)] = jnp.broadcast_to(top(p_den), pk_own.shape)[None]
    for d in range(1, n_ty):
        rdma(pk_c.at[ty], pk_c.at[ty], msend.at[d], mrecv.at[ty], {"ty": (ty + d) % n_ty}).start()
    for dx in (-1, 1):
        @pl.when(present(0, dx, shape))
        def _():
            for dy in (-1, 1):
                fold_h(-dx, dy).wait_recv()
    for dx in (-1, 1):
        at = edge_part(dx, inner, margin)
        for dy in (-1, 1):
            part_rows = pl.ds(*wide_part(dy, rows, half))
            tot[:, pl.ds(*at), part_rows, :] += landing(0, -dx)[:, :, part_rows, :]
    start_folds_v((2, 3))
    num_chain.step4()
    full = num_chain.result()
    p_re, p_im = full[:each], full[each:]

    for dx in (-1, 1):
        @pl.when(present(0, dx, shape))
        def _():
            for dy in (-1, 1, 0):
                fold_h(dx, dy).wait_send()
            fold_h(-dx, 0).wait_recv()
    for dy in (-1, 1):
        @pl.when(present(dy, 0, shape))
        def _():
            for i in range(len(groups)):
                fold_v(dy, i).wait_send()
                fold_v(-dy, i).wait_recv()

    for d in range(1, n_ty):
        o = (ty + d) % n_ty
        rdma(pk_b.at[ty], pk_b.at[o], lsend.at[d], lrecv.at[o], {"ty": o}).wait()
    peak = pk_b[0]
    for t in range(1, n_ty):
        peak = jnp.maximum(peak, pk_b[t])
    den[...] = 1.0 / (den[...] + 0.1 * peak[0:1, 0:1])

    for j in range(inner):
        for ch in range(2):
            for r in range(0, rows, chunk):
                inside = slice(half + r, half + r + chunk)
                value = tot[ch, j + margin, inside, :]
                if r < half:
                    value = value + landing(1, 0)[ch, j, r:r + chunk, :]
                if r >= rows - half:
                    value = value + landing(-1, 0)[ch, j, r - rows + half:r - rows + half + chunk, :]
                if j < margin:
                    value = value + landing(0, 1)[ch, j, inside, :]
                if j >= inner - margin:
                    value = value + landing(0, -1)[ch, j - inner + margin, inside, :]
                own = wide[ch, j + margin, inside, :]
                out[ch, r:r + chunk, j * LANES:(j + 1) * LANES] = own + value * den[j, r:r + chunk, :]

    for d in range(1, n_ty):
        o = (ty + d) % n_ty
        rdma(pk_c.at[ty], pk_c.at[o], msend.at[d], mrecv.at[o], {"ty": o}).wait()
    peak = pk_c[0]
    for t in range(1, n_ty):
        peak = jnp.maximum(peak, pk_c[t])
    scale = 1.0 / (p_den + 0.1 * peak[0:1, 0:1])
    own_rows = pl.ds(pl.multiple_of(ty * each, each), each)
    out_probe[0] = probe[0, own_rows, :] + p_re * scale
    out_probe[1] = probe[1, own_rows, :] + p_im * scale


def finish_kernel(tile, probe, out, out_probe, sems):
    copies = [
        pltpu.make_async_copy(tile, out, sems.at[0]),
        pltpu.make_async_copy(probe, out_probe, sems.at[1])]
    for copy in copies:
        copy.start()
    for copy in copies:
        copy.wait()


def table_values(length):
    half = length // 2
    j, m = np.arange(half), np.arange(half)
    even = 2.0 * math.pi / length * (np.outer(2 * m, j) % length)
    odd = 2.0 * math.pi / length * (np.outer(2 * m + 1, j) % length)
    values = []
    for phase in (even, odd, odd.T):
        values += [np.cos(phase) / math.sqrt(length), np.sin(phase) / math.sqrt(length)]
    high = [value.astype(jnp.bfloat16) for value in values]
    low = [(value - h.astype(np.float64)).astype(jnp.bfloat16) for value, h in zip(values, high)]
    return np.stack(high + low)


def body(shape, object_slices, probe_field, positions, live_slots, photon_counts):
    f32 = jnp.float32
    dma = pltpu.SemaphoreType.DMA
    size = probe_field.shape[1]
    half = size // 2
    tile = object_slices[0]
    _, rows, cols = tile.shape
    spots = positions[0, 0, 0].T
    slots = spots.shape[1]
    inner, margin = cols // LANES, half // LANES
    blocks = inner + 2 * margin
    span = size // LANES + 1
    n_ty, n_tx, n_an = shape["ty"], shape["tx"], shape["angle"]
    n_z, each, group = n_ty // 2, size // n_ty, n_an * n_tx
    part = size // n_an
    vmem = pl.BlockSpec(memory_space=pltpu.VMEM)
    smem = pl.BlockSpec(memory_space=pltpu.SMEM)
    hbm = pl.BlockSpec(memory_space=pltpu.HBM)

    def chain_scratch(height):
        return [
            pltpu.VMEM((2, n_z, height, size), f32),
            pltpu.VMEM((n_z, height, size), f32),
            pltpu.VMEM((n_z, height, size), f32),
            pltpu.VMEM((n_an, n_z, height, part), f32),
            pltpu.VMEM((n_z, height, part), f32),
            pltpu.VMEM((n_z, height, part), f32),
            pltpu.VMEM((height, part), f32),
            pltpu.VMEM((group, height, part), f32),
            dma((1,)), dma((1,)), dma((n_an,)), dma((n_an,)), dma((n_z,)), dma((n_z,)), dma((group,)), dma((group,)),
        ]

    new_tile, new_probe = pl.pallas_call(
        functools.partial(step_kernel, shape),
        out_shape=(
            jax.ShapeDtypeStruct((2, rows, cols), f32),
            jax.ShapeDtypeStruct((2, each, size), f32),
        ),
        in_specs=[smem, hbm, hbm, hbm, hbm, hbm],
        out_specs=(vmem, vmem),
        scratch_shapes=[
            pltpu.SMEM(spots.shape, jnp.int32),
            pltpu.VMEM((2, blocks, rows + size, LANES), f32),
            pltpu.VMEM((2, blocks, rows + size, LANES), f32),
            pltpu.VMEM((inner, rows, LANES), f32),
            pltpu.VMEM((slots, 2, span + 2, rows + 2 * size, LANES), f32),
            pltpu.VMEM((9, 8, LANES), jnp.int32),
            pltpu.SMEM((9, 8, LANES), jnp.int32),
            pltpu.VMEM((2, size, size), f32),
            pltpu.VMEM((slots, size // LANES, size, LANES), jnp.int32),
            pltpu.VMEM((slots, size, size), f32),
            pltpu.VMEM((12, half, half), jnp.bfloat16),
            pltpu.VMEM((2, 4, size, size), jnp.bfloat16),
            pltpu.VMEM((slots, 2, size, size), f32),
            pltpu.VMEM((2, 2, inner, half, LANES), f32),
            pltpu.VMEM((2, 2, margin, rows + size, LANES), f32),
            pltpu.VMEM((8, LANES), f32),
            pltpu.VMEM((group, 8, LANES), f32),
            pltpu.VMEM((n_ty, 8, LANES), f32),
            pltpu.VMEM((n_ty, 8, LANES), f32),
            dma((12,)), dma((12,)), dma((9,)), dma((9,)),
            dma((14,)), dma((14,)),
            dma((group,)), dma((group,)), dma((n_ty,)), dma((n_ty,)), dma((n_ty,)), dma((n_ty,)),
            dma((4 + size // LANES,)), dma((inner,)),
            *chain_scratch(each), *chain_scratch(2 * each),
        ],
        compiler_params=pltpu.CompilerParams(
            collective_id=0, has_side_effects=True, vmem_limit_bytes=VMEM_LIMIT),
    )(live_slots[0], *[
        pltpu.with_memory_space_constraint(value, pltpu.HBM)
        for value in (spots, tile, probe_field, photon_counts[0, 0, 0], jnp.asarray(table_values(size)))])

    return pl.pallas_call(
        finish_kernel,
        out_shape=(
            jax.ShapeDtypeStruct(new_tile.shape, f32),
            jax.ShapeDtypeStruct(new_probe.shape, f32),
        ),
        in_specs=[vmem, vmem],
        out_specs=(hbm, hbm),
        scratch_shapes=[dma((2,))],
        compiler_params=pltpu.CompilerParams(vmem_limit_bytes=FINISH_LIMIT),
    )(new_tile, new_probe)


def solution(mesh):
    shape = dict(mesh.shape)

    def step(*args):
        new_tile, new_probe = body(shape, *args)
        return new_tile[None], new_probe

    return jax.shard_map(
        step,
        mesh=mesh,
        in_specs=(
            P("angle", None, "ty", "tx"),
            P(),
            P("angle", "ty", "tx", None, None),
            P("angle", "ty", "tx"),
            P("angle", "ty", "tx", None, None, None),
        ),
        out_specs=(P("angle", None, "ty", "tx"), P(None, "ty", None)),
        check_vma=False,
    )
```

time: 63.7 us -> 49.6 us (0.78)
  Pallas kernels: 58.1 us -> 48.1 us
  local copies, waits for them, and re-layouts: 3.82 us -> 0 us
    pallas_call x1, Pallas kernels: 58.1 us -> 46.7 us  [body(): pl.pallas_call(functools.partial(step_kernel, shape), out_shape=(jax.Shap...]
    unnamed x4 -> x0, local copies, waits for them, and re-layouts: 3.82 us -> none
    pallas_call x0 -> x1, Pallas kernels: none -> 1.34 us  [body(): pl.pallas_call(finish_kernel, out_shape=(jax.ShapeDtypeStruct(new_tile.sh...]
where the time goes in v1:
time: 49.6 us; the launch traced here: 49.4 us
  Pallas kernels  48.1 us (97%)
  between operations  1.29 us (3%)
    pallas_call x1, Pallas kernels, body(): pl.pallas_call(functools.partial(step_kernel, shape), out_shape=(jax.Shap...  46.7 us
    pallas_call x1, Pallas kernels, body(): pl.pallas_call(finish_kernel, out_shape=(jax.ShapeDtypeStruct(new_tile.sh...  1.34 us

profile of v1, /device:TPU:1, one launch (start us, length us, event | category | flops | bytes accessed | tf_op | source)
XLA Modules:
  0.0 49.4 jit_solution(11539212841128505135)
XLA Ops:
  1.3 46.7 %shard_map.77 = (f32[2,256,1024]{2,1,0:T(8,128)S(1)}, f32[2,32,256]{2,1,0:T(8,128)S(1)}) custom-call(s32[1,1]{1,0:T(1,128)} %bitcast.7.live, s32[2,4]{1,0:T(2,128)} %bitcast.10, f32[2,256,1024]{2,1,0:T(8,128)} %bitcast.8, f32[2,256,256]{2,1,0:T(8,128)} %probe_in.1, s32[4,256,256]{2,1,0:T(8,128)} %bitcast.9, bf16[12,128,128]{2,1,0:T(8,128)(2,1)} %constant.2.clone.tables_in), custom_call_target="tpu_custom_call" | custom-call | tf_op jit(solution)/shard_map/pallas_call | solution.py:676
  48.0 1.3 %shard_map.78 = (f32[2,256,1024]{2,1,0:T(8,128)}, f32[2,32,256]{2,1,0:T(8,128)}) custom-call(f32[2,256,1024]{2,1,0:T(8,128)S(1)} %get-tuple-element.6.tile, f32[2,32,256]{2,1,0:T(8,128)S(1)} %get-tuple-element.7.probe), custom_call_target="tpu_custom_call" | custom-call | tf_op jit(solution)/shard_map/pallas_call | solution.py:716

commit v2 on v1

--- a/solution.py
+++ b/solution.py
@@ -70,7 +70,7 @@
         shape, live, pos_in, tile_in, probe_in, counts_in, tables_in,
         out, out_probe,
         pos, wide, tot, den, dbuf, metas, smetas, probe, counts, amp, tables, mats,
-        xbuf, rim_v, rim_h, pk_own, pk_a, pk_b, pk_c,
+        xbuf, rim_v, rim_h, pair_h, pk_own, pk_a, pk_b, pk_c,
         hsend, hrecv, nsend, nrecv, fsend, frecv, ksend, krecv, lsend, lrecv, msend, mrecv, local, local_tile,
         *chain_refs):
     f32 = jnp.float32
@@ -109,6 +109,35 @@
     for copy in load_tile + load_counts + [load_probe, load_tables]:
         copy.start()
 
+    for k in range(9):
+        if k != 4:
+            metas[k] = jnp.zeros((8, LANES), jnp.int32)
+    barrier = pltpu.get_barrier_semaphore()
+
+    def signal(where):
+        pl.semaphore_signal(barrier, inc=1, device_id=where, device_id_type=MESH)
+
+    def member(d):
+        g = (gid + d) % group
+        return g, {"angle": g // n_tx, "tx": g % n_tx}
+
+    for d in range(1, n_ty):
+        signal({"ty": (ty + d) % n_ty})
+    for d in range(1, group):
+        signal(member(d)[1])
+    for dy, dx in DIAGONALS:
+        @pl.when(present(dy, dx, shape))
+        def _():
+            signal(neighbour(dy, dx))
+    outer_dy, inner_dy = 2 * core - 1, 1 - 2 * core
+    outer_there = (ty + outer_dy >= 0) & (ty + outer_dy < n_ty)
+    outer_at = pl.multiple_of(core * (half + rows), 8)
+    shared_at = pl.multiple_of(half + (1 - core) * (rows - half), 8)
+    inner_at = pl.multiple_of((1 - core) * (half + rows), 8)
+
+    def beside(dx):
+        return (tx + dx >= 0) & (tx + dx < n_tx)
+
     load_pos.wait()
     lane8 = lax.broadcasted_iota(jnp.int32, (8, LANES), 1)
     line = jnp.zeros((8, LANES), jnp.int32)
@@ -116,40 +145,64 @@
         line = jnp.where(lane8 == s, pos[0, s], line)
         line = jnp.where(lane8 == slots + s, pos[1, s], line)
     line = jnp.where(lane8 == 2 * slots, live[0, 0], line)
-    for k in range(9):
-        metas[k] = line if k == 4 else jnp.zeros((8, LANES), jnp.int32)
-
-    barrier = pltpu.get_barrier_semaphore()
-
-    def signal(where):
-        pl.semaphore_signal(barrier, inc=1, device_id=where, device_id_type=MESH)
-
-    def member(d):
-        g = (gid + d) % group
-        return g, {"angle": g // n_tx, "tx": g % n_tx}
-
-    for d in range(1, n_ty):
-        signal({"ty": (ty + d) % n_ty})
-    for d in range(1, group):
-        signal(member(d)[1])
-    for dy, dx in DIAGONALS:
+    metas[4] = line
+
+    for copy in load_tile:
+        copy.wait()
+    n_row, n_col = beside_counts(shape)
+    pl.semaphore_wait(barrier, n_ty - 1 + group - 1 + n_row * n_col)
+
+    def rdma(src, dst, s_sem, r_sem, where):
+        return pltpu.make_async_remote_copy(
+            src_ref=src, dst_ref=dst, send_sem=s_sem, recv_sem=r_sem,
+            device_id=where, device_id_type=MESH)
+
+    strips = ((margin, margin), (inner, margin), (2 * margin, inner - 2 * margin))
+    SIDES = ((-1, 0), (1, 0), (0, -1), (0, 1))
+
+    def halo_v(dy, i):
+        src = region(wide, edge_part(dy, rows, half), strips[i])
+        dst = region(wide, wide_part(-dy, rows, half), strips[i])
+        k = (dy + 1) // 2 * len(strips) + i
+        return rdma(src, dst, hsend.at[k], hrecv.at[k], neighbour(dy, 0))
+
+    def halo_h(dx, dy):
+        part_rows = wide_part(dy, rows, half)
+        src = region(wide, part_rows, edge_part(dx, inner, margin))
+        dst = region(wide, part_rows, wide_part(-dx, inner, margin))
+        k = 2 * len(strips) + (dx + 1) // 2 * 3 + dy + 1
+        return rdma(src, dst, hsend.at[k], hrecv.at[k], neighbour(0, dx))
+
+    def note(dy, dx):
+        k = slot_of(dy, dx)
+        return rdma(metas.at[4], metas.at[slot_of(-dy, -dx)], nsend.at[k], nrecv.at[k], neighbour(dy, dx))
+
+    order = sorted(BESIDE, key=lambda d: abs(d[1]))
+    for dy, dx in order:
         @pl.when(present(dy, dx, shape))
         def _():
-            signal(neighbour(dy, dx))
-    def landing(dy, dx):
-        return rim_v.at[(dy + 1) // 2] if dx == 0 else rim_h.at[(dx + 1) // 2]
-
-    for dy, dx in ((-1, 0), (1, 0), (0, -1), (0, 1)):
-        @pl.when(jnp.logical_not(present(dy, dx, shape)))
-        def _():
-            place = landing(-dy, -dx)
-            place[...] = jnp.zeros(place.shape, f32)
-
-    for dy, dx in BESIDE:
-        @pl.when(jnp.logical_not(present(dy, dx, shape)))
-        def _():
-            place = landing(-dy, -dx)
-            place[...] = jnp.zeros(place.shape, f32)
+            note(dy, dx).start()
+    for dy, dx in SIDES:
+        @pl.when(present(dy, dx, shape))
+        def _():
+            if dx == 0:
+                halo_v(dy, 0).start()
+                halo_v(dy, 1).start()
+            else:
+                halo_h(dx, 0).start()
+    for dy in (-1, 1):
+        @pl.when(present(dy, 0, shape))
+        def _():
+            halo_v(dy, 2).start()
+
+    @pl.when(jnp.logical_not(outer_there))
+    def _():
+        rim_v[0] = jnp.zeros(rim_v.shape[1:], f32)
+
+    for side, dx in enumerate((-1, 1)):
+        @pl.when(jnp.logical_not(beside(dx)))
+        def _():
+            rim_h[side] = jnp.zeros(rim_h.shape[1:], f32)
 
     def clear(n, carry):
         s, ch = n // 2, n % 2
@@ -174,54 +227,6 @@
             mats[n, m, 0:half, half:] = up
             mats[n, m, half:, 0:half] = down
             mats[n, m, half:, half:] = c
-
-    for copy in load_tile:
-        copy.wait()
-    n_row, n_col = beside_counts(shape)
-    pl.semaphore_wait(barrier, n_ty - 1 + group - 1 + n_row * n_col)
-
-    def rdma(src, dst, s_sem, r_sem, where):
-        return pltpu.make_async_remote_copy(
-            src_ref=src, dst_ref=dst, send_sem=s_sem, recv_sem=r_sem,
-            device_id=where, device_id_type=MESH)
-
-    strips = ((margin, margin), (inner, margin), (2 * margin, inner - 2 * margin))
-    SIDES = ((-1, 0), (1, 0), (0, -1), (0, 1))
-
-    def halo_v(dy, i):
-        src = region(wide, edge_part(dy, rows, half), strips[i])
-        dst = region(wide, wide_part(-dy, rows, half), strips[i])
-        k = (dy + 1) // 2 * len(strips) + i
-        return rdma(src, dst, hsend.at[k], hrecv.at[k], neighbour(dy, 0))
-
-    def halo_h(dx, dy):
-        part_rows = wide_part(dy, rows, half)
-        src = region(wide, part_rows, edge_part(dx, inner, margin))
-        dst = region(wide, part_rows, wide_part(-dx, inner, margin))
-        k = 2 * len(strips) + (dx + 1) // 2 * 3 + dy + 1
-        return rdma(src, dst, hsend.at[k], hrecv.at[k], neighbour(0, dx))
-
-    def note(dy, dx):
-        k = slot_of(dy, dx)
-        return rdma(metas.at[4], metas.at[slot_of(-dy, -dx)], nsend.at[k], nrecv.at[k], neighbour(dy, dx))
-
-    order = sorted(BESIDE, key=lambda d: abs(d[1]))
-    for dy, dx in order:
-        @pl.when(present(dy, dx, shape))
-        def _():
-            note(dy, dx).start()
-    for dy, dx in SIDES:
-        @pl.when(present(dy, dx, shape))
-        def _():
-            if dx == 0:
-                halo_v(dy, 0).start()
-                halo_v(dy, 1).start()
-            else:
-                halo_h(dx, 0).start()
-    for dy in (-1, 1):
-        @pl.when(present(dy, 0, shape))
-        def _():
-            halo_v(dy, 2).start()
 
     for copy in load_counts:
         copy.wait()
@@ -355,10 +360,15 @@
         found = mm(cat([high, low, high], 1), matrix(m, 0))
         return found[:, :half], found[:, half:]
 
-    def add_to(total, s, values):
+    def add_to(total, values):
+        cut = total.shape[3]
+        length = min(cut, each)
         for t in range(n_ty):
             for ch, value in enumerate(values):
-                total[t % 2, t // 2, ch * each:(ch + 1) * each, :] += value[t * each:(t + 1) * each, :]
+                for i in range(0, each, length):
+                    at = ch * each + i
+                    total[t % 2, t // 2, at // cut, at % cut:at % cut + length, :] += (
+                        value[t * each + i:t * each + i + length, :])
 
     def extract(s, carry):
         row, first, shift = place(4, s)
@@ -372,39 +382,46 @@
                 for b in range(span)]
             found.append(cat([jnp.where(keep, moved[b], moved[b + 1]) for b in range(pieces)], 1))
             xbuf[s, ch] = found[ch]
-        add_to(sums_d, s, (jnp.where(used, found[0] * found[0] + found[1] * found[1], 0.0),))
+        add_to(sums_d, (jnp.where(used, found[0] * found[0] + found[1] * found[1], 0.0),))
         return carry
 
-    def one_slot(s, carry):
+    def slot_steps(s):
         shift = place(4, s)[2]
         used = s < smetas[4, 0, 2 * slots]
-        x_re, x_im = xbuf[s, 0], xbuf[s, 1]
-        q_re, q_im = probe[0], probe[1]
-        p_re = q_re * x_re - q_im * x_im
-        p_im = q_re * x_im + q_im * x_re
+
+        def psi():
+            x_re, x_im = xbuf[s, 0], xbuf[s, 1]
+            q_re, q_im = probe[0], probe[1]
+            return q_re * x_re - q_im * x_im, q_re * x_im + q_im * x_re
+
+        p_re, p_im = psi()
         a = from_left(0, p_re[:half] + p_re[half:], p_im[:half] + p_im[half:])
         b = from_left(1, p_re[:half] - p_re[half:], p_im[:half] - p_im[half:])
+        yield
         y_re, y_im = cat([a[0], b[0]], 0), cat([a[1], b[1]], 0)
         a = from_right(2, y_re[:, :half] + y_re[:, half:], y_im[:, :half] + y_im[:, half:])
         b = from_right(3, y_re[:, :half] - y_re[:, half:], y_im[:, :half] - y_im[:, half:])
+        yield
         f_re, f_im = cat([a[0], b[0]], 1), cat([a[1], b[1]], 1)
         factor = amp[s] * lax.rsqrt(jnp.maximum(f_re * f_re + f_im * f_im, 0.0625))
         g_re, g_im = f_re * factor, f_im * factor
         a = from_left(2, g_re[:half], g_im[:half])
         b = from_left(3, g_re[half:], g_im[half:])
+        yield
         y_re, y_im = cat([a[0] + b[0], a[0] - b[0]], 0), cat([a[1] + b[1], a[1] - b[1]], 0)
         a = from_right(0, y_re[:, :half], y_im[:, :half])
         b = from_right(1, y_re[:, half:], y_im[:, half:])
+        yield
+        p_re, p_im = psi()
         b_re, b_im = cat([a[0] + b[0], a[0] - b[0]], 1), cat([a[1] + b[1], a[1] - b[1]], 1)
         d_re, d_im = jnp.where(used, b_re - p_re, 0.0), jnp.where(used, b_im - p_im, 0.0)
+        x_re, x_im = xbuf[s, 0], xbuf[s, 1]
+        q_re, q_im = probe[0], probe[1]
         for ch, value in enumerate((q_re * d_re + q_im * d_im, q_re * d_im - q_im * d_re)):
             for i, moved in enumerate(spread(value, shift)):
                 dbuf[s, ch, 1 + i, size:2 * size, :] = moved
-        add_to(sums_n, s, (x_re * d_re + x_im * d_im, x_re * d_im - x_im * d_re))
-        return carry
-
-    def lanes(ref, a):
-        return ref.at[:, :, pl.ds(pl.multiple_of(a * part, part), part)]
+        add_to(sums_n, (x_re * d_re + x_im * d_im, x_re * d_im - x_im * d_re))
+        yield
 
     class Chain:
         def __init__(self, refs):
@@ -414,17 +431,17 @@
         def pair(self):
             return rdma(self.sums.at[1 - core], self.r1, self.send1.at[0], self.recv1.at[0], {"ty": ty + 1 - 2 * core})
 
-        def over_angle(self, d, get):
-            a = (an + d) % n_an
+        def over_plane(self, d, get):
+            g, where = member(d)
+            at = g if get else gid
+            lanes = pl.ds(pl.multiple_of(g // n_tx * part, part), part)
             return rdma(
-                lanes(self.s1, a), self.r2.at[a if get else an], self.send2.at[d],
-                self.recv2.at[a if get else an], {"angle": a})
+                self.s1.at[:, g % n_tx, :, lanes], self.r2.at[at], self.send2.at[d], self.recv2.at[at], where)
 
         def over_z(self, d, get):
             o = (z + d) % n_z
-            return rdma(
-                self.s2.at[o], self.r3.at[o if get else z], self.send3.at[d],
-                self.recv3.at[o if get else z], {"ty": o * 2 + core})
+            at = o if get else z
+            return rdma(self.s2.at[o], self.r3.at[at], self.send3.at[d], self.recv3.at[at], {"ty": o * 2 + core})
 
         def over_group(self, d, get):
             g, where = member(d)
@@ -437,15 +454,15 @@
         def step2(self):
             self.pair().wait()
             self.s1[...] = self.sums[core] + self.r1[...]
-            for d in range(1, n_an):
-                self.over_angle(d, False).start()
+            for d in range(1, group):
+                self.over_plane(d, False).start()
 
         def step3(self):
-            for d in range(1, n_an):
-                self.over_angle(d, True).wait()
-            total = self.s1[:, :, pl.ds(pl.multiple_of(an * part, part), part)]
-            for d in range(1, n_an):
-                total = total + self.r2[(an + d) % n_an]
+            for d in range(1, group):
+                self.over_plane(d, True).wait()
+            total = self.s1[:, tx, :, pl.ds(pl.multiple_of(an * part, part), part)]
+            for d in range(1, group):
+                total = total + self.r2[(gid + d) % group]
             self.s2[...] = total
             for d in range(1, n_z):
                 self.over_z(d, False).start()
@@ -464,28 +481,22 @@
         def result(self):
             for d in range(1, group):
                 self.over_group(d, True).wait()
-            found = []
-            for a in range(n_an):
-                piece = self.g4[a * n_tx]
-                for t in range(1, n_tx):
-                    piece = piece + self.g4[a * n_tx + t]
-                found.append(piece)
-            return cat(found, 1)
+            return cat([cat([self.g4[a * n_tx + t] for t in range(n_tx)], 0) for a in range(n_an)], 1)
 
     den_chain, num_chain = Chain(den_refs), Chain(num_refs)
+
     def some_slots(*which):
-        for s in which:
-            one_slot(s, 0)
+        running = [slot_steps(s) for s in which]
+        for _ in range(5):
+            for steps in running:
+                next(steps)
 
     lax.fori_loop(0, slots, extract, 0)
     den_chain.step1()
-    some_slots(0)
+    some_slots(*range(slots // 2))
     den_chain.step2()
-    some_slots(*range(1, slots - 1))
-    den_chain.step3()
-    some_slots(slots - 1)
+    some_slots(*range(slots // 2, slots))
     num_chain.step1()
-
     for d in range(1, group):
         g, where = member(d)
         rdma(pk_own, pk_a.at[g], ksend.at[d], krecv.at[g], where).wait()
@@ -500,88 +511,135 @@
         def column(n, carry):
             j = lowest + n // 2
             ch = n % 2
-            for r in range(start, start + count, chunk):
-                tot[ch, j, r:r + chunk, :] = gathered(ch, j, r, chunk, spots)
+            for r in range(0, count, chunk):
+                at = start + r if isinstance(start, int) else pl.multiple_of(start + r, 8)
+                tot[ch, j, pl.ds(at, chunk), :] = gathered(ch, j, at, chunk, spots)
             return carry
 
         lax.fori_loop(0, 2 * number, column, 0)
 
-    def fold_h(dx, dy):
-        part_rows = wide_part(dy, rows, half)
-        k = (dx + 1) // 2 * 3 + dy + 1
+    middle = inner - 2 * margin
+    third = middle // 3
+    groups = (
+        (2 * margin, third), (2 * margin + third, third), (2 * margin + 2 * third, middle - 2 * third),
+        (margin, margin), (inner, margin))
+
+    def fold_outer(i):
+        start, count = groups[i]
         return rdma(
-            region(tot, part_rows, wide_part(dx, inner, margin)),
-            landing(0, dx).at[:, :, pl.ds(*part_rows), :], fsend.at[k], frecv.at[k], neighbour(0, dx))
-
-    middle = inner - 2 * margin
-    first = middle * 2 // 3
-    groups = ((2 * margin, first), (2 * margin + first, middle - first), (margin, margin), (inner, margin))
-
-    def fold_v(dy, i):
-        start, count = groups[i]
-        k = 6 + (dy + 1) // 2 * len(groups) + i
+            region(tot, (outer_at, half), groups[i]), rim_v.at[0, :, pl.ds(start - margin, count)],
+            fsend.at[i], frecv.at[i], {"ty": ty + outer_dy})
+
+    def fold_inner():
         return rdma(
-            region(tot, wide_part(dy, rows, half), groups[i]),
-            landing(dy, 0).at[:, pl.ds(start - margin, count)], fsend.at[k], frecv.at[k], neighbour(dy, 0))
-
-    def start_folds_v(which):
-        for dy in (-1, 1):
-            @pl.when(present(dy, 0, shape))
-            def _():
-                for i in which:
-                    fold_v(dy, i).start()
-
-    def start_folds_h(which):
-        for dx in (-1, 1):
-            @pl.when(present(0, dx, shape))
-            def _():
-                for dy in which:
-                    fold_h(dx, dy).start()
-
-    total_at(0, half, margin, inner)
-    total_at(half + rows, half, margin, inner)
-    start_folds_v((0,))
-    total_at(0, 2 * half + rows, 0, margin)
-    total_at(0, 2 * half + rows, margin + inner, margin)
-    start_folds_h((-1,))
+            region(tot, (inner_at, half), (margin, inner)), rim_v.at[1], fsend.at[13], frecv.at[13], {"ty": ty + inner_dy})
+
+    def side_of(dx):
+        return wide_part(dx, inner, margin)
+
+    def fold_beside(dx, n):
+        k = 5 + (dx + 1) // 2 + 6 * n
+        start = shared_at if n else pl.multiple_of(half + core * half, 8)
+        count = half if n else rows - half
+        return rdma(
+            region(tot, (start, count), side_of(dx)),
+            rim_h.at[(1 - dx) // 2, :, :, pl.ds(pl.multiple_of(start - half, 8), count)],
+            fsend.at[k], frecv.at[k], {"tx": tx + dx})
+
+    def fold_corner(dx):
+        k = 7 + (dx + 1) // 2
+        return rdma(
+            region(tot, (outer_at, half), side_of(dx)), rim_h.at[(1 - dx) // 2, :, :, pl.ds(rows, half)],
+            fsend.at[k], frecv.at[k], {"tx": tx + dx})
+
+    def fold_pair(dx):
+        k = 9 + (dx + 1) // 2
+        return rdma(
+            region(tot, (inner_at, half), side_of(dx)), pair_h.at[(dx + 1) // 2],
+            fsend.at[k], frecv.at[k], {"ty": ty + inner_dy})
+
+    @pl.when(outer_there)
+    def _():
+        total_at(outer_at, half, *groups[0])
+        fold_outer(0).start()
+
+    for dx in (-1, 1):
+        @pl.when(beside(dx))
+        def _():
+            total_at(inner_at, half, *side_of(dx))
+            fold_pair(dx).start()
+            total_at(outer_at, half, *side_of(dx))
+            total_at(half, rows, *side_of(dx))
     num_chain.step2()
+    for dx in (-1, 1):
+        @pl.when(beside(dx) & outer_there)
+        def _():
+            fold_corner(dx).start()
+    den_chain.step3()
+    @pl.when(outer_there)
+    def _():
+        total_at(outer_at, half, *groups[1])
+        fold_outer(1).start()
+        for i in (2, 3, 4):
+            total_at(outer_at, half, *groups[i])
+
+    total_at(inner_at, half, margin, inner)
+    fold_inner().start()
     total_at(half, rows, margin, inner)
+    num_chain.step3()
+
+    @pl.when(outer_there)
+    def _():
+        fold_outer(2).start()
+
     den_chain.step4()
-    start_folds_h((1, 0))
-    num_chain.step3()
-    start_folds_v((1,))
+    for dx in (-1, 1):
+        @pl.when(beside(dx))
+        def _():
+            fold_beside(dx, 0).start()
+    for dx in (-1, 1):
+        @pl.when(beside(dx) & outer_there)
+        def _():
+            fold_corner(-dx).wait_recv()
+            start, count = edge_part(dx, inner, margin)
+            tot[:, pl.ds(start, count), pl.ds(outer_at, half), :] += rim_h[(dx + 1) // 2, :, :, rows:, :]
+
+    @pl.when(outer_there)
+    def _():
+        fold_outer(3).start()
+        fold_outer(4).start()
+
     p_den = den_chain.result()
     pk_c[pl.ds(ty, 1)] = jnp.broadcast_to(top(p_den), pk_own.shape)[None]
     for d in range(1, n_ty):
         rdma(pk_c.at[ty], pk_c.at[ty], msend.at[d], mrecv.at[ty], {"ty": (ty + d) % n_ty}).start()
+    num_chain.step4()
     for dx in (-1, 1):
-        @pl.when(present(0, dx, shape))
-        def _():
-            for dy in (-1, 1):
-                fold_h(-dx, dy).wait_recv()
-    for dx in (-1, 1):
-        at = edge_part(dx, inner, margin)
-        for dy in (-1, 1):
-            part_rows = pl.ds(*wide_part(dy, rows, half))
-            tot[:, pl.ds(*at), part_rows, :] += landing(0, -dx)[:, :, part_rows, :]
-    start_folds_v((2, 3))
-    num_chain.step4()
+        @pl.when(beside(dx))
+        def _():
+            fold_pair(dx).wait()
+            tot[:, pl.ds(*side_of(dx)), pl.ds(shared_at, half), :] += pair_h[(dx + 1) // 2]
+            fold_beside(dx, 1).start()
     full = num_chain.result()
     p_re, p_im = full[:each], full[each:]
 
     for dx in (-1, 1):
-        @pl.when(present(0, dx, shape))
-        def _():
-            for dy in (-1, 1, 0):
-                fold_h(dx, dy).wait_send()
-            fold_h(-dx, 0).wait_recv()
-    for dy in (-1, 1):
-        @pl.when(present(dy, 0, shape))
-        def _():
-            for i in range(len(groups)):
-                fold_v(dy, i).wait_send()
-                fold_v(-dy, i).wait_recv()
-
+        @pl.when(beside(dx))
+        def _():
+            for n in range(2):
+                fold_beside(dx, n).wait_send()
+                fold_beside(-dx, n).wait_recv()
+
+        @pl.when(beside(dx) & outer_there)
+        def _():
+            fold_corner(dx).wait_send()
+
+    @pl.when(outer_there)
+    def _():
+        for i in range(len(groups)):
+            fold_outer(i).wait()
+
+    fold_inner().wait()
     for d in range(1, n_ty):
         o = (ty + d) % n_ty
         rdma(pk_b.at[ty], pk_b.at[o], lsend.at[d], lrecv.at[o], {"ty": o}).wait()
@@ -596,13 +654,13 @@
                 inside = slice(half + r, half + r + chunk)
                 value = tot[ch, j + margin, inside, :]
                 if r < half:
-                    value = value + landing(1, 0)[ch, j, r:r + chunk, :]
+                    value = value + rim_v[core, ch, j, r:r + chunk, :]
                 if r >= rows - half:
-                    value = value + landing(-1, 0)[ch, j, r - rows + half:r - rows + half + chunk, :]
+                    value = value + rim_v[1 - core, ch, j, r - rows + half:r - rows + half + chunk, :]
                 if j < margin:
-                    value = value + landing(0, 1)[ch, j, inside, :]
+                    value = value + rim_h[0, ch, j, r:r + chunk, :]
                 if j >= inner - margin:
-                    value = value + landing(0, -1)[ch, j - inner + margin, inside, :]
+                    value = value + rim_h[1, ch, j - inner + margin, r:r + chunk, :]
                 own = wide[ch, j + margin, inside, :]
                 out[ch, r:r + chunk, j * LANES:(j + 1) * LANES] = own + value * den[j, r:r + chunk, :]
 
@@ -661,16 +719,17 @@
     hbm = pl.BlockSpec(memory_space=pltpu.HBM)
 
     def chain_scratch(height):
+        cut = height // n_tx
         return [
-            pltpu.VMEM((2, n_z, height, size), f32),
-            pltpu.VMEM((n_z, height, size), f32),
-            pltpu.VMEM((n_z, height, size), f32),
-            pltpu.VMEM((n_an, n_z, height, part), f32),
-            pltpu.VMEM((n_z, height, part), f32),
-            pltpu.VMEM((n_z, height, part), f32),
-            pltpu.VMEM((height, part), f32),
-            pltpu.VMEM((group, height, part), f32),
-            dma((1,)), dma((1,)), dma((n_an,)), dma((n_an,)), dma((n_z,)), dma((n_z,)), dma((group,)), dma((group,)),
+            pltpu.VMEM((2, n_z, n_tx, cut, size), f32),
+            pltpu.VMEM((n_z, n_tx, cut, size), f32),
+            pltpu.VMEM((n_z, n_tx, cut, size), f32),
+            pltpu.VMEM((group, n_z, cut, part), f32),
+            pltpu.VMEM((n_z, cut, part), f32),
+            pltpu.VMEM((n_z, cut, part), f32),
+            pltpu.VMEM((cut, part), f32),
+            pltpu.VMEM((group, cut, part), f32),
+            dma((1,)), dma((1,)), dma((group,)), dma((group,)), dma((n_z,)), dma((n_z,)), dma((group,)), dma((group,)),
         ]
 
     new_tile, new_probe = pl.pallas_call(
@@ -696,7 +755,8 @@
             pltpu.VMEM((2, 4, size, size), jnp.bfloat16),
             pltpu.VMEM((slots, 2, size, size), f32),
             pltpu.VMEM((2, 2, inner, half, LANES), f32),
-            pltpu.VMEM((2, 2, margin, rows + size, LANES), f32),
+            pltpu.VMEM((2, 2, margin, rows + half, LANES), f32),
+            pltpu.VMEM((2, 2, margin, half, LANES), f32),
             pltpu.VMEM((8, LANES), f32),
             pltpu.VMEM((group, 8, LANES), f32),
             pltpu.VMEM((n_ty, 8, LANES), f32),

time: 49.6 us -> 45.9 us (0.925)
  Pallas kernels: 48.1 us -> 44 us
    pallas_call x1, Pallas kernels: 46.7 us -> 42.7 us  [body(): pl.pallas_call(functools.partial(step_kernel, shape), out_shape=(jax.Shap...]
where the time goes in v2:
time: 45.9 us; the launch traced here: 45.3 us
  Pallas kernels  44 us (96%)
  between operations  1.29 us (3%)
    pallas_call x1, Pallas kernels, body(): pl.pallas_call(functools.partial(step_kernel, shape), out_shape=(jax.Shap...  42.7 us
    pallas_call x1, Pallas kernels, body(): pl.pallas_call(finish_kernel, out_shape=(jax.ShapeDtypeStruct(new_tile.sh...  1.34 us

profile of v2, /device:TPU:1, one launch (start us, length us, event | category | flops | bytes accessed | tf_op | source)
XLA Modules:
  0.0 45.3 jit_solution(6829908665848678450)
XLA Ops:
  1.3 42.7 %shard_map.77 = (f32[2,256,1024]{2,1,0:T(8,128)S(1)}, f32[2,32,256]{2,1,0:T(8,128)S(1)}) custom-call(s32[1,1]{1,0:T(1,128)} %bitcast.7.live, s32[2,4]{1,0:T(2,128)} %bitcast.10, f32[2,256,1024]{2,1,0:T(8,128)} %bitcast.8, f32[2,256,256]{2,1,0:T(8,128)} %probe_in.1, s32[4,256,256]{2,1,0:T(8,128)} %bitcast.9, bf16[12,128,128]{2,1,0:T(8,128)(2,1)} %constant.2.clone.tables_in), custom_call_target="tpu_custom_call" | custom-call | tf_op jit(solution)/shard_map/pallas_call | solution.py:735
  44.0 1.3 %shard_map.78 = (f32[2,256,1024]{2,1,0:T(8,128)}, f32[2,32,256]{2,1,0:T(8,128)}) custom-call(f32[2,256,1024]{2,1,0:T(8,128)S(1)} %get-tuple-element.6.tile, f32[2,32,256]{2,1,0:T(8,128)S(1)} %get-tuple-element.7.probe), custom_call_target="tpu_custom_call" | custom-call | tf_op jit(solution)/shard_map/pallas_call | solution.py:776

commit v3 on v2

--- a/solution.py
+++ b/solution.py
@@ -11,7 +11,7 @@
 
 MESH = pl.DeviceIdType.MESH
 LANES = 128
-VMEM_LIMIT = 44 * 1024 * 1024
+VMEM_LIMIT = 40 * 1024 * 1024
 FINISH_LIMIT = 4 * 1024 * 1024
 AROUND = tuple((dy, dx) for dy in (-1, 0, 1) for dx in (-1, 0, 1))
 BESIDE = tuple(d for d in AROUND if d != (0, 0))
@@ -68,9 +68,9 @@
 
 def step_kernel(
         shape, live, pos_in, tile_in, probe_in, counts_in, tables_in,
-        out, out_probe,
-        pos, wide, tot, den, dbuf, metas, smetas, probe, counts, amp, tables, mats,
-        xbuf, rim_v, rim_h, pair_h, pk_own, pk_a, pk_b, pk_c,
+        wide, tot, den, rim_v, rim_h, out_probe,
+        pos, dbuf, metas, smetas, probe, counts, amp, tables, mats,
+        xbuf, pair_h, pk_own, pk_a, pk_b, pk_c,
         hsend, hrecv, nsend, nrecv, fsend, frecv, ksend, krecv, lsend, lrecv, msend, mrecv, local, local_tile,
         *chain_refs):
     f32 = jnp.float32
@@ -485,17 +485,18 @@
 
     den_chain, num_chain = Chain(den_refs), Chain(num_refs)
 
-    def some_slots(*which):
+    def some_slots(which, between):
         running = [slot_steps(s) for s in which]
-        for _ in range(5):
+        for n in range(5):
             for steps in running:
                 next(steps)
+            if n in between:
+                between[n]()
 
     lax.fori_loop(0, slots, extract, 0)
     den_chain.step1()
-    some_slots(*range(slots // 2))
-    den_chain.step2()
-    some_slots(*range(slots // 2, slots))
+    some_slots(range(slots // 2), {3: den_chain.step2})
+    some_slots(range(slots // 2, slots), {})
     num_chain.step1()
     for d in range(1, group):
         g, where = member(d)
@@ -597,6 +598,10 @@
         @pl.when(beside(dx))
         def _():
             fold_beside(dx, 0).start()
+    p_den = den_chain.result()
+    pk_c[pl.ds(ty, 1)] = jnp.broadcast_to(top(p_den), pk_own.shape)[None]
+    for d in range(1, n_ty):
+        rdma(pk_c.at[ty], pk_c.at[ty], msend.at[d], mrecv.at[ty], {"ty": (ty + d) % n_ty}).start()
     for dx in (-1, 1):
         @pl.when(beside(dx) & outer_there)
         def _():
@@ -609,10 +614,6 @@
         fold_outer(3).start()
         fold_outer(4).start()
 
-    p_den = den_chain.result()
-    pk_c[pl.ds(ty, 1)] = jnp.broadcast_to(top(p_den), pk_own.shape)[None]
-    for d in range(1, n_ty):
-        rdma(pk_c.at[ty], pk_c.at[ty], msend.at[d], mrecv.at[ty], {"ty": (ty + d) % n_ty}).start()
     num_chain.step4()
     for dx in (-1, 1):
         @pl.when(beside(dx))
@@ -647,22 +648,6 @@
     for t in range(1, n_ty):
         peak = jnp.maximum(peak, pk_b[t])
     den[...] = 1.0 / (den[...] + 0.1 * peak[0:1, 0:1])
-
-    for j in range(inner):
-        for ch in range(2):
-            for r in range(0, rows, chunk):
-                inside = slice(half + r, half + r + chunk)
-                value = tot[ch, j + margin, inside, :]
-                if r < half:
-                    value = value + rim_v[core, ch, j, r:r + chunk, :]
-                if r >= rows - half:
-                    value = value + rim_v[1 - core, ch, j, r - rows + half:r - rows + half + chunk, :]
-                if j < margin:
-                    value = value + rim_h[0, ch, j, r:r + chunk, :]
-                if j >= inner - margin:
-                    value = value + rim_h[1, ch, j - inner + margin, r:r + chunk, :]
-                own = wide[ch, j + margin, inside, :]
-                out[ch, r:r + chunk, j * LANES:(j + 1) * LANES] = own + value * den[j, r:r + chunk, :]
 
     for d in range(1, n_ty):
         o = (ty + d) % n_ty
@@ -676,14 +661,32 @@
     out_probe[1] = probe[1, own_rows, :] + p_im * scale
 
 
-def finish_kernel(tile, probe, out, out_probe, sems):
-    copies = [
-        pltpu.make_async_copy(tile, out, sems.at[0]),
-        pltpu.make_async_copy(probe, out_probe, sems.at[1])]
-    for copy in copies:
-        copy.start()
+def finish_kernel(wide, tot, den, rim_v, rim_h, probe, out, out_probe, held, sems, probe_sem):
+    core = lax.axis_index("ty") % 2
+    inner, rows, _ = den.shape
+    margin, half = rim_h.shape[2], rim_v.shape[3]
+    keep_probe = pltpu.make_async_copy(probe, out_probe, probe_sem.at[0])
+    keep_probe.start()
+    copies = []
+    for j in range(inner):
+        for ch in range(2):
+            for r in range(0, rows, half):
+                inside = slice(half + r, half + r + half)
+                value = tot[ch, j + margin, inside, :]
+                if r < half:
+                    value = value + rim_v[core, ch, j, r:r + half, :]
+                if r >= rows - half:
+                    value = value + rim_v[1 - core, ch, j, r - rows + half:r - rows + 2 * half, :]
+                if j < margin:
+                    value = value + rim_h[0, ch, j, r:r + half, :]
+                if j >= inner - margin:
+                    value = value + rim_h[1, ch, j - inner + margin, r:r + half, :]
+                held[j, ch, r:r + half, :] = wide[ch, j + margin, inside, :] + value * den[j, r:r + half, :]
+        copies.append(pltpu.make_async_copy(held.at[j], out.at[:, :, pl.ds(j * LANES, LANES)], sems.at[j]))
+        copies[-1].start()
     for copy in copies:
         copy.wait()
+    keep_probe.wait()
 
 
 def table_values(length):
@@ -732,19 +735,20 @@
             dma((1,)), dma((1,)), dma((group,)), dma((group,)), dma((n_z,)), dma((n_z,)), dma((group,)), dma((group,)),
         ]
 
-    new_tile, new_probe = pl.pallas_call(
+    *parts, new_probe = pl.pallas_call(
         functools.partial(step_kernel, shape),
-        out_shape=(
-            jax.ShapeDtypeStruct((2, rows, cols), f32),
-            jax.ShapeDtypeStruct((2, each, size), f32),
-        ),
+        out_shape=[pltpu.VMEM(size_of, f32) for size_of in (
+            (2, blocks, rows + size, LANES),
+            (2, blocks, rows + size, LANES),
+            (inner, rows, LANES),
+            (2, 2, inner, half, LANES),
+            (2, 2, margin, rows + half, LANES),
+            (2, each, size),
+        )],
         in_specs=[smem, hbm, hbm, hbm, hbm, hbm],
-        out_specs=(vmem, vmem),
+        out_specs=[vmem] * 6,
         scratch_shapes=[
             pltpu.SMEM(spots.shape, jnp.int32),
-            pltpu.VMEM((2, blocks, rows + size, LANES), f32),
-            pltpu.VMEM((2, blocks, rows + size, LANES), f32),
-            pltpu.VMEM((inner, rows, LANES), f32),
             pltpu.VMEM((slots, 2, span + 2, rows + 2 * size, LANES), f32),
             pltpu.VMEM((9, 8, LANES), jnp.int32),
             pltpu.SMEM((9, 8, LANES), jnp.int32),
@@ -754,8 +758,6 @@
             pltpu.VMEM((12, half, half), jnp.bfloat16),
             pltpu.VMEM((2, 4, size, size), jnp.bfloat16),
             pltpu.VMEM((slots, 2, size, size), f32),
-            pltpu.VMEM((2, 2, inner, half, LANES), f32),
-            pltpu.VMEM((2, 2, margin, rows + half, LANES), f32),
             pltpu.VMEM((2, 2, margin, half, LANES), f32),
             pltpu.VMEM((8, LANES), f32),
             pltpu.VMEM((group, 8, LANES), f32),
@@ -776,14 +778,14 @@
     return pl.pallas_call(
         finish_kernel,
         out_shape=(
-            jax.ShapeDtypeStruct(new_tile.shape, f32),
-            jax.ShapeDtypeStruct(new_probe.shape, f32),
+            jax.ShapeDtypeStruct((2, rows, cols), f32),
+            jax.ShapeDtypeStruct((2, each, size), f32),
         ),
-        in_specs=[vmem, vmem],
+        in_specs=[vmem] * 6,
         out_specs=(hbm, hbm),
-        scratch_shapes=[dma((2,))],
+        scratch_shapes=[pltpu.VMEM((inner, 2, rows, LANES), f32), dma((inner,)), dma((1,))],
         compiler_params=pltpu.CompilerParams(vmem_limit_bytes=FINISH_LIMIT),
-    )(new_tile, new_probe)
+    )(*parts, new_probe)
 
 
 def solution(mesh):

time: 45.9 us -> 45.3 us (0.987)
  no operation moved by 1% of the time
where the time goes in v3:
time: 45.3 us; the launch traced here: 45.1 us
  Pallas kernels  43.9 us (97%)
  between operations  1.28 us (3%)
    pallas_call x1, Pallas kernels, body(): pl.pallas_call(functools.partial(step_kernel, shape), out_shape=[pltpu.VM...  42.4 us
    pallas_call x1, Pallas kernels, body(): pl.pallas_call(finish_kernel, out_shape=(jax.ShapeDtypeStruct((2, rows, c...  1.45 us

profile of v3, /device:TPU:1, one launch (start us, length us, event | category | flops | bytes accessed | tf_op | source)
XLA Modules:
  0.0 45.1 jit_solution(14059966972477312454)
XLA Ops:
  1.3 42.4 %shard_map.77 = (f32[2,10,512,128]{3,2,1,0:T(8,128)S(1)}, f32[2,10,512,128]{3,2,1,0:T(8,128)S(1)}, f32[8,256,128]{2,1,0:T(8,128)S(1)}, f32[2,2,8,128,128]{4,3,2,...) custom-call(s32[1,1]{1,0:T(1,128)} %bitcast.7.live, s32[2,4]{1,0:T(2,128)} %bitcast.10, ...), custom_call_target="tpu_custom_call" | custom-call | tf_op jit(solution)/shard_map/pallas_call | solution.py:738
  43.7 1.5 %shard_map.78 = (f32[2,256,1024]{2,1,0:T(8,128)}, f32[2,32,256]{2,1,0:T(8,128)}) custom-call(f32[2,10,512,128]{3,2,1,0:T(8,128)S(1)} %get-tuple-element.10.wide, f32[2,10,512,128]{3,2,1,0:T(8,128)S(1)} %get-tuple-element.11.tot, f32[8,256,128]{2,1,0:T(8,128)S(1)} %get-tuple-element.12.den, f32[2,2,8,128,128]{4,3,2,1,0:T(8,128)S(1)} %get-tuple-element.13.rim_v, ...), custom_call_target="tpu_custom_call" | custom-call | tf_op jit(solution)/shard_map/pallas_call | solution.py:778

commit v4 on v3

--- a/solution.py
+++ b/solution.py
@@ -118,8 +118,8 @@
         pl.semaphore_signal(barrier, inc=1, device_id=where, device_id_type=MESH)
 
     def member(d):
-        g = (gid + d) % group
-        return g, {"angle": g // n_tx, "tx": g % n_tx}
+        a, t = (an + d // n_tx) % n_an, (tx + d % n_tx) % n_tx
+        return a * n_tx + t, {"angle": a, "tx": t}
 
     for d in range(1, n_ty):
         signal({"ty": (ty + d) % n_ty})
@@ -454,7 +454,7 @@
         def step2(self):
             self.pair().wait()
             self.s1[...] = self.sums[core] + self.r1[...]
-            for d in range(1, group):
+            for d in reversed(range(1, group)):
                 self.over_plane(d, False).start()
 
         def step3(self):
@@ -475,7 +475,7 @@
                 total = total + self.r3[(z + d) % n_z]
             self.s3[...] = total
             self.g4[pl.ds(gid, 1)] = total[None]
-            for d in range(1, group):
+            for d in reversed(range(1, group)):
                 self.over_group(d, False).start()
 
         def result(self):
@@ -621,26 +621,6 @@
             fold_pair(dx).wait()
             tot[:, pl.ds(*side_of(dx)), pl.ds(shared_at, half), :] += pair_h[(dx + 1) // 2]
             fold_beside(dx, 1).start()
-    full = num_chain.result()
-    p_re, p_im = full[:each], full[each:]
-
-    for dx in (-1, 1):
-        @pl.when(beside(dx))
-        def _():
-            for n in range(2):
-                fold_beside(dx, n).wait_send()
-                fold_beside(-dx, n).wait_recv()
-
-        @pl.when(beside(dx) & outer_there)
-        def _():
-            fold_corner(dx).wait_send()
-
-    @pl.when(outer_there)
-    def _():
-        for i in range(len(groups)):
-            fold_outer(i).wait()
-
-    fold_inner().wait()
     for d in range(1, n_ty):
         o = (ty + d) % n_ty
         rdma(pk_b.at[ty], pk_b.at[o], lsend.at[d], lrecv.at[o], {"ty": o}).wait()
@@ -648,6 +628,26 @@
     for t in range(1, n_ty):
         peak = jnp.maximum(peak, pk_b[t])
     den[...] = 1.0 / (den[...] + 0.1 * peak[0:1, 0:1])
+    full = num_chain.result()
+    p_re, p_im = full[:each], full[each:]
+
+    for dx in (-1, 1):
+        @pl.when(beside(dx))
+        def _():
+            for n in range(2):
+                fold_beside(dx, n).wait_send()
+                fold_beside(-dx, n).wait_recv()
+
+        @pl.when(beside(dx) & outer_there)
+        def _():
+            fold_corner(dx).wait_send()
+
+    @pl.when(outer_there)
+    def _():
+        for i in range(len(groups)):
+            fold_outer(i).wait()
+
+    fold_inner().wait()
 
     for d in range(1, n_ty):
         o = (ty + d) % n_ty

time: 45.3 us -> 45.1 us (level)
  no operation moved by 1% of the time
where the time goes in v4:
time: 45.1 us; the launch traced here: 45 us
  Pallas kernels  43.7 us (97%)
  between operations  1.28 us (3%)
    pallas_call x1, Pallas kernels, body(): pl.pallas_call(functools.partial(step_kernel, shape), out_shape=[pltpu.VM...  42.2 us
    pallas_call x1, Pallas kernels, body(): pl.pallas_call(finish_kernel, out_shape=(jax.ShapeDtypeStruct((2, rows, c...  1.45 us

profile of v4, /device:TPU:1, one launch (start us, length us, event | category | flops | bytes accessed | tf_op | source)
XLA Modules:
  0.0 45.0 jit_solution(12992532932946561925)
XLA Ops:
  1.3 42.2 %shard_map.77 = (f32[2,10,512,128]{3,2,1,0:T(8,128)S(1)}, f32[2,10,512,128]{3,2,1,0:T(8,128)S(1)}, f32[8,256,128]{2,1,0:T(8,128)S(1)}, f32[2,2,8,128,128]{4,3,2,...) custom-call(s32[1,1]{1,0:T(1,128)} %bitcast.7.live, s32[2,4]{1,0:T(2,128)} %bitcast.10, ...), custom_call_target="tpu_custom_call" | custom-call | tf_op jit(solution)/shard_map/pallas_call | solution.py:738
  43.5 1.5 %shard_map.78 = (f32[2,256,1024]{2,1,0:T(8,128)}, f32[2,32,256]{2,1,0:T(8,128)}) custom-call(f32[2,10,512,128]{3,2,1,0:T(8,128)S(1)} %get-tuple-element.10.wide, f32[2,10,512,128]{3,2,1,0:T(8,128)S(1)} %get-tuple-element.11.tot, f32[8,256,128]{2,1,0:T(8,128)S(1)} %get-tuple-element.12.den, f32[2,2,8,128,128]{4,3,2,1,0:T(8,128)S(1)} %get-tuple-element.13.rim_v, ...), custom_call_target="tpu_custom_call" | custom-call | tf_op jit(solution)/shard_map/pallas_call | solution.py:778
